TPU v7x, 512 devices: a whole 4x4x16 slice. The times are simulated.
512 devices in a mesh: phase: 8 (over y, core), wide: 64 (over x, z).
Axes of the slice: x: 4, y: 4, z: 16, core: 2. Of those that a mesh axis runs over, the one named last changes fastest.
Arguments:
- image: bfloat16 [16, 256, 16384], P(None, None, 'wide'), may hold values from -6 to 6
- conv_weight: bfloat16 [8, 256, 2304], P('phase'), may hold values from -0.09375 to 0.09375
- class_weight: bfloat16 [11, 256], replicated, may hold values from -0.375 to 0.375
- point_feats: float32 [16, 4, 16384], P('phase', None, 'wide'), may hold values from -6 to 6
- pixel_index: int32 [16, 16384], P('phase', 'wide'), may hold values from 0 to 16383
- pillar_index: int32 [16, 16384], P('phase', 'wide'), may hold values from 0 to 8191
- point_counts: int32 [16, 64], P('phase', 'wide'), may hold values from 64 to 256, as said below
- pillar_weight: float32 [64, 15], replicated, may hold values from -1.5 to 1.5
- bev_weight: bfloat16 [576, 384], replicated, may hold values from -0.25 to 0.25
- head_weight: bfloat16 [384, 20], replicated, may hold values from -0.3125 to 0.3125
Outputs:
- detections: float32 [16, 8192, 20], P('phase', 'wide')
- scores: float32 [16, 11, 16384], P('phase', None, 'wide')
Inputs may be any that keep to these rules, and one draw needn't show every extreme that they name: `point_counts`: in every frame some index of wide has all 256 slots live; slots at or past the count are padding.
All inputs are finite; a program needn't handle non-finite values.
Results may differ from a plain program's by a relative error of at most 0.01.
Values may be sent and summed in bfloat16 or wider, within the bound.
A program may use at most 64 MiB of HBM per device.

v0:
```python
import jax
import jax.numpy as jnp
from jax import lax
from jax.sharding import Mesh
from jax.sharding import PartitionSpec as P

PIL = 64
HEAD = 384
IMG_W = 64
BEV_W = 128
CELLS_DEV = 128
WIDE = ("wide_0", "wide_1")


def padded_2(value, sides, width):
    for axis, dim in sides:
        devices, length = (lax.axis_size(axis), value.shape[dim])
        up = [(i, (i + 1) % devices) for i in range(devices - 1)]
        down = [(j, i) for i, j in up]
        last = lax.slice_in_dim(value, length - width, length, axis=dim)
        first = lax.slice_in_dim(value, 0, width, axis=dim)
        before = lax.ppermute(last, axis, up)
        after = lax.ppermute(first, axis, down)
        value = jnp.concatenate([before, value, after], axis=dim)
    return value


def joined_along(parts, dim):
    dims = list(parts.shape[1:])
    dims[dim] *= parts.shape[0]
    return jnp.moveaxis(parts, 0, dim).reshape(dims)


def copy_for_each(value, axis):
    devices = lax.axis_size(axis)
    return lax.all_to_all(
        jnp.broadcast_to(value[None], (devices, *value.shape)), axis, 0, 0, tiled=True
    )


def gather_directly(value, axis, dim):
    return joined_along(copy_for_each(value, axis), dim)


def whole_of(value, axes, dim):
    filled = value
    for number in range(len(axes) - 1, -1, -1):
        filled = lax.all_gather(filled, axes[number], axis=dim, tiled=True)
    return filled


def image_layer(activation, weight):
    length = activation.shape[2]
    padded = padded_2(activation, ((WIDE, 2),), IMG_W)
    extended = jnp.pad(padded, ((0, 0), (0, 0), (1, 1)))
    column = jnp.arange(length, dtype=jnp.int32) % IMG_W
    sections = []
    for row_step in range(3):
        for col_step in range(3):
            offset = row_step * IMG_W + col_step
            section = lax.slice_in_dim(extended, offset, offset + length, axis=2)
            inside = (column + col_step - 1 >= 0) & (column + col_step - 1 < IMG_W)
            sections.append(jnp.where(inside[None, None, :], section, jnp.zeros_like(section)))
    stacked = jnp.concatenate(sections, axis=1)
    summed = jnp.einsum("ok,fkp->fop", weight, stacked, preferred_element_type=jnp.float32)
    return (activation.astype(jnp.float32) + jax.nn.relu(summed)).astype(jnp.bfloat16)


def bev_layer(grid, bev_weight, own_frames):
    padded = padded_2(grid, ((WIDE, 0),), BEV_W)
    extended = jnp.pad(padded, ((1, 1), (0, 0)))
    column = jnp.arange(CELLS_DEV, dtype=jnp.int32) % BEV_W
    sections = []
    for row_step in range(3):
        for col_step in range(3):
            offset = row_step * BEV_W + col_step
            section = lax.slice_in_dim(extended, offset, offset + CELLS_DEV, axis=0)
            inside = (column + col_step - 1 >= 0) & (column + col_step - 1 < BEV_W)
            sections.append(jnp.where(inside[:, None], section, jnp.zeros_like(section)))
    stacked = jnp.stack(sections, axis=1).reshape(CELLS_DEV, 9, own_frames, PIL)
    summed = jnp.einsum(
        "ctfj,tjo->fco",
        stacked,
        bev_weight.reshape(9, PIL, HEAD),
        preferred_element_type=jnp.float32,
    )
    return jax.nn.relu(summed).astype(jnp.bfloat16)


def local(
    image,
    conv_weight,
    class_weight,
    point_feats,
    pixel_index,
    pillar_index,
    point_counts,
    pillar_weight,
    bev_weight,
    head_weight,
):
    phase_now = lax.axis_index("phase")
    phases = lax.axis_size("phase")
    own_frames = point_feats.shape[0]
    weights = lax.all_gather(conv_weight, "phase", axis=0, tiled=True)
    start_maps = lax.dynamic_slice_in_dim(image, phase_now * own_frames, own_frames, 0)

    def layer_step(layer, activation):
        return image_layer(activation, lax.dynamic_index_in_dim(weights, layer, 0, keepdims=False))

    own_maps = lax.fori_loop(0, phases, layer_step, start_maps)
    scores = jnp.einsum("kc,fcp->fkp", class_weight, own_maps, preferred_element_type=jnp.float32)
    logits = scores.astype(jnp.bfloat16)
    section = gather_directly(logits, WIDE, 2)
    extent = section.shape[2]
    onehot = (pixel_index[:, None, :] == jnp.arange(extent, dtype=jnp.int32)[None, :, None]).astype(
        jnp.bfloat16
    )
    painted = jnp.einsum("fkn,fnp->fkp", section, onehot, preferred_element_type=jnp.float32)
    features = jnp.concatenate([point_feats, jax.nn.sigmoid(painted)], axis=1)
    hidden = jax.nn.relu(
        jnp.einsum("jd,fdp->fjp", pillar_weight, features, precision=lax.Precision.HIGHEST)
    )
    positions = jnp.arange(pixel_index.shape[1], dtype=jnp.int32)
    is_live = positions[None, :] < point_counts
    hidden = jnp.where(is_live[:, None, :], hidden, 0.0).astype(jnp.bfloat16)
    own_first = lax.axis_index(WIDE) * CELLS_DEV
    part_hidden = whole_of(hidden, ("wide_1", "wide_0"), 2)
    part_index = whole_of(pillar_index[:, None, :], ("wide_1", "wide_0"), 2)
    onehot = (
        part_index[:, 0, :, None] - own_first
        == jnp.arange(CELLS_DEV, dtype=jnp.int32)[None, None, :]
    ).astype(jnp.bfloat16)
    partial_sum = jnp.einsum(
        "fjp,fpc->cfj", part_hidden, onehot, preferred_element_type=jnp.float32
    )
    pooled = partial_sum.reshape(CELLS_DEV, own_frames * PIL)
    grid = pooled.astype(jnp.bfloat16)
    feature = bev_layer(grid, bev_weight, own_frames)
    detections = jnp.einsum("fco,or->fcr", feature, head_weight, preferred_element_type=jnp.float32)
    return (detections, scores)


def solution(mesh):
    finer = Mesh(mesh.devices.reshape(mesh.shape["phase"], 4, 16), ("phase", "wide_0", "wide_1"))
    placed = (
        P(None, None, WIDE),
        P("phase", None, None),
        P(),
        P("phase", None, WIDE),
        P("phase", WIDE),
        P("phase", WIDE),
        P("phase", WIDE),
        P(),
        P(),
        P(),
    )
    return jax.shard_map(
        local,
        mesh=finer,
        in_specs=placed,
        out_specs=(P("phase", WIDE, None), P("phase", None, WIDE)),
        check_vma=False,
    )
```

profile of v0, /device:TPU:6, one launch (start us, length us, event | category | flops | bytes accessed | tf_op | source)
XLA Modules:
  0.0 344.1 jit_solution(6971880708646652760)
XLA Ops:
  8.9 67.4 %all-gather.5.cloned.1.call-done = bf16[8,256,2304]{2,1,0:T(8,128)(2,1)} async-done(((bf16[1,256,2304]{2,1,0:T(8,128)(2,1)}), bf16[8,256,2304]{2,1,0:T(8,128)(2,1)}) %all-gather.5.cloned.1.call-update) | async-done | bytes 9437200 | tf_op jit(solution)/shard_map/all_gather | solution.py:105
  76.3 112.8 %while.18 = (s32[]{:T(128)}, bf16[2,256,256]{1,2,0:T(8,128)(2,1)S(1)}, bf16[8,256,2304]{2,1,0:T(8,128)(2,1)}, s32[]{:T(128)}) while((s32[]{:T(128)}, bf16[2,256,256]{1,2,0:T(8,128)(2,1)S(1)}, bf16[8,256,2304]{2,1,0:T(8,128)(2,1)}, s32[]{:T(128)}) %tuple.72), condition=%wide.region_1.2_spmd, body=%wide.region_0.1_spmd.sunk | while | flops 608062720 | bytes 11410577 | solution.py:111
  76.3 6.2 %collective-permute-start = (bf16[2,256,64]{1,2,0:T(8,128)(2,1)S(1)}, bf16[2,256,64]{1,2,0:T(8,128)(2,1)S(1)}, u32[]{:S(2)}, u32[]{:S(2)}) collective-permute-start(bf16[2,256,64]{1,2,0:T(8,128)(2,1)S(1)} %get-tuple-element.195), channel_id=1, source_target_pairs={{1,0},{2,1},{3,2},{4,3},{5,4},{6,5},{7,6},{8,7},{9,8},{10,9},{11,1... | collective-permute-start | bytes 196616 | tf_op jit(solution)/shard_map/while/body/eval_jaxpr/ppermute | solution.py:23
  84.5 6.3 %collective-permute-done.1 = bf16[2,256,64]{1,2,0:T(8,128)(2,1)S(1)} collective-permute-done((bf16[2,256,64]{1,2,0:T(8,128)(2,1)S(1)}, bf16[2,256,64]{1,2,0:T(8,128)(2,1)S(1)}, u32[]{:S(2)}, u32[]{:S(2)}) %collective-permute-start.1) | collective-permute-done | bytes 65568 | tf_op jit(solution)/shard_map/while/body/eval_jaxpr/ppermute | solution.py:22
  96.1 3.9 %collective-permute-start.1 = (bf16[2,256,64]{1,2,0:T(8,128)(2,1)S(1)}, bf16[2,256,64]{1,2,0:T(8,128)(2,1)S(1)}, u32[]{:S(2)}, u32[]{:S(2)}) collective-permute-start(bf16[2,256,64]{1,2,0:T(8,128)(2,1)S(1)} %get-tuple-element.196), channel_id=1, source_target_pairs={{0,1},{1,2},{2,3},{3,4},{4,5},{5,6},{6,7},{7,8},{8,9},{9,10},{10,1... | collective-permute-start | bytes 196616 | tf_op jit(solution)/shard_map/while/body/eval_jaxpr/ppermute | solution.py:22
  100.1 4.3 %collective-permute-done.1 = bf16[2,256,64]{1,2,0:T(8,128)(2,1)S(1)} collective-permute-done((bf16[2,256,64]{1,2,0:T(8,128)(2,1)S(1)}, bf16[2,256,64]{1,2,0:T(8,128)(2,1)S(1)}, u32[]{:S(2)}, u32[]{:S(2)}) %collective-permute-start.1) | collective-permute-done | bytes 65568 | tf_op jit(solution)/shard_map/while/body/eval_jaxpr/ppermute | solution.py:22
  109.7 3.9 %collective-permute-start.1 = (bf16[2,256,64]{1,2,0:T(8,128)(2,1)S(1)}, bf16[2,256,64]{1,2,0:T(8,128)(2,1)S(1)}, u32[]{:S(2)}, u32[]{:S(2)}) collective-permute-start(bf16[2,256,64]{1,2,0:T(8,128)(2,1)S(1)} %get-tuple-element.196), channel_id=1, source_target_pairs={{0,1},{1,2},{2,3},{3,4},{4,5},{5,6},{6,7},{7,8},{8,9},{9,10},{10,1... | collective-permute-start | bytes 196616 | tf_op jit(solution)/shard_map/while/body/eval_jaxpr/ppermute | solution.py:22
  113.7 4.3 %collective-permute-done.1 = bf16[2,256,64]{1,2,0:T(8,128)(2,1)S(1)} collective-permute-done((bf16[2,256,64]{1,2,0:T(8,128)(2,1)S(1)}, bf16[2,256,64]{1,2,0:T(8,128)(2,1)S(1)}, u32[]{:S(2)}, u32[]{:S(2)}) %collective-permute-start.1) | collective-permute-done | bytes 65568 | tf_op jit(solution)/shard_map/while/body/eval_jaxpr/ppermute | solution.py:22
  123.3 3.9 %collective-permute-start.1 = (bf16[2,256,64]{1,2,0:T(8,128)(2,1)S(1)}, bf16[2,256,64]{1,2,0:T(8,128)(2,1)S(1)}, u32[]{:S(2)}, u32[]{:S(2)}) collective-permute-start(bf16[2,256,64]{1,2,0:T(8,128)(2,1)S(1)} %get-tuple-element.196), channel_id=1, source_target_pairs={{0,1},{1,2},{2,3},{3,4},{4,5},{5,6},{6,7},{7,8},{8,9},{9,10},{10,1... | collective-permute-start | bytes 196616 | tf_op jit(solution)/shard_map/while/body/eval_jaxpr/ppermute | solution.py:22
  127.2 4.3 %collective-permute-done.1 = bf16[2,256,64]{1,2,0:T(8,128)(2,1)S(1)} collective-permute-done((bf16[2,256,64]{1,2,0:T(8,128)(2,1)S(1)}, bf16[2,256,64]{1,2,0:T(8,128)(2,1)S(1)}, u32[]{:S(2)}, u32[]{:S(2)}) %collective-permute-start.1) | collective-permute-done | bytes 65568 | tf_op jit(solution)/shard_map/while/body/eval_jaxpr/ppermute | solution.py:22
  136.8 3.9 %collective-permute-start.1 = (bf16[2,256,64]{1,2,0:T(8,128)(2,1)S(1)}, bf16[2,256,64]{1,2,0:T(8,128)(2,1)S(1)}, u32[]{:S(2)}, u32[]{:S(2)}) collective-permute-start(bf16[2,256,64]{1,2,0:T(8,128)(2,1)S(1)} %get-tuple-element.196), channel_id=1, source_target_pairs={{0,1},{1,2},{2,3},{3,4},{4,5},{5,6},{6,7},{7,8},{8,9},{9,10},{10,1... | collective-permute-start | bytes 196616 | tf_op jit(solution)/shard_map/while/body/eval_jaxpr/ppermute | solution.py:22
  140.8 4.3 %collective-permute-done.1 = bf16[2,256,64]{1,2,0:T(8,128)(2,1)S(1)} collective-permute-done((bf16[2,256,64]{1,2,0:T(8,128)(2,1)S(1)}, bf16[2,256,64]{1,2,0:T(8,128)(2,1)S(1)}, u32[]{:S(2)}, u32[]{:S(2)}) %collective-permute-start.1) | collective-permute-done | bytes 65568 | tf_op jit(solution)/shard_map/while/body/eval_jaxpr/ppermute | solution.py:22
  154.4 4.3 %collective-permute-done.1 = bf16[2,256,64]{1,2,0:T(8,128)(2,1)S(1)} collective-permute-done((bf16[2,256,64]{1,2,0:T(8,128)(2,1)S(1)}, bf16[2,256,64]{1,2,0:T(8,128)(2,1)S(1)}, u32[]{:S(2)}, u32[]{:S(2)}) %collective-permute-start.1) | collective-permute-done | bytes 65568 | tf_op jit(solution)/shard_map/while/body/eval_jaxpr/ppermute | solution.py:22
  167.9 4.3 %collective-permute-done.1 = bf16[2,256,64]{1,2,0:T(8,128)(2,1)S(1)} collective-permute-done((bf16[2,256,64]{1,2,0:T(8,128)(2,1)S(1)}, bf16[2,256,64]{1,2,0:T(8,128)(2,1)S(1)}, u32[]{:S(2)}, u32[]{:S(2)}) %collective-permute-start.1) | collective-permute-done | bytes 65568 | tf_op jit(solution)/shard_map/while/body/eval_jaxpr/ppermute | solution.py:22
  181.5 4.3 %collective-permute-done.1 = bf16[2,256,64]{1,2,0:T(8,128)(2,1)S(1)} collective-permute-done((bf16[2,256,64]{1,2,0:T(8,128)(2,1)S(1)}, bf16[2,256,64]{1,2,0:T(8,128)(2,1)S(1)}, u32[]{:S(2)}, u32[]{:S(2)}) %collective-permute-start.1) | collective-permute-done | bytes 65568 | tf_op jit(solution)/shard_map/while/body/eval_jaxpr/ppermute | solution.py:22
  191.2 5.4 %all-to-all-start = ((bf16[64,2,11,256]{3,1,2,0:T(2,128)(2,1)}), bf16[64,2,11,256]{3,1,2,0:T(2,128)(2,1)S(1)}, u32[]{:S(2)}, u32[]{:S(2)}) async-start(bf16[64,2,11,256]{3,1,2,0:T(2,128)(2,1)} %broadcast_in_dim.201), calls=%async_computation | async-start | bytes 1441792 | tf_op jit(solution)/shard_map/all_to_all | solution.py:36
  196.8 29.8 %all-to-all-done = bf16[64,2,11,256]{3,1,2,0:T(2,128)(2,1)S(1)} async-done(((bf16[64,2,11,256]{3,1,2,0:T(2,128)(2,1)}), bf16[64,2,11,256]{3,1,2,0:T(2,128)(2,1)S(1)}, u32[]{:S(2)}, u32[]{:S(2)}) %all-to-all-start) | async-done | bytes 720928 | tf_op jit(solution)/shard_map/all_to_all | solution.py:36
  228.2 6.5 %fusion.35 = f32[2,11,256]{2,1,0:T(8,128)S(1)} fusion(bf16[2,11,16384]{2,1,0:T(8,128)(2,1)} %reshape.132, s32[2,256]{1,0:T(2,128)S(1)} %copy-done.7), kind=kOutput, calls=%fused_computation.59 | convolution fusion | flops 192954880 | bytes 745472 | tf_op jit(solution)/shard_map/fkn,fnp->fkp/dot_general | solution.py:119
  235.1 13.0 %all_gather.18 = bf16[2,64,1024]{2,1,0:T(8,128)(2,1)} all-gather(bf16[2,64,256]{2,1,0:T(8,128)(2,1)S(1)} %fusion.30), channel_id=1, replica_groups=mesh['phase'=8,'wide_0'=4,'wide_1'=16] {'wide_0'}, dimensions={2}, use_global_device_ids=true | all-gather | bytes 327680 | tf_op jit(solution)/shard_map/all_gather | solution.py:48
  248.1 10.2 %all-gather = s32[2,1024]{1,0:T(2,128)S(1)} all-gather(s32[2,256]{1,0:T(2,128)S(1)} %copy-done.4), channel_id=2, replica_groups=mesh['phase'=8,'wide_0'=4,'wide_1'=16] {'wide_0'}, dimensions={1}, use_global_device_ids=true | all-gather | bytes 10240 | tf_op jit(solution)/shard_map/all_gather | solution.py:48
  258.3 29.0 %all-gather.1 = s32[2,16384]{1,0:T(2,128)S(1)} all-gather(s32[2,1024]{1,0:T(2,128)S(1)} %all-gather), channel_id=3, replica_groups=mesh['phase'=8,'wide_0'=4,'wide_1'=16] {'wide_1'}, dimensions={1}, use_global_device_ids=true | all-gather | bytes 139264 | tf_op jit(solution)/shard_map/all_gather | solution.py:48
  287.4 31.9 %all-gather.7.cloned.1.call-done = bf16[2,64,16384]{2,1,0:T(8,128)(2,1)} async-done(((bf16[2,64,1024]{2,1,0:T(8,128)(2,1)}), bf16[2,64,16384]{2,1,0:T(8,128)(2,1)}) %all-gather.7.cloned.1.call-update) | async-done | bytes 4194320 | tf_op jit(solution)/shard_map/all_gather | solution.py:48
  319.3 6.7 %fusion.31 = bf16[2,128,64]{1,2,0:T(8,128)(2,1)S(1)} fusion(bf16[2,64,16384]{2,1,0:T(8,128)(2,1)} %all-gather.7.cloned.1.call-done, s32[2,16384]{1,0:T(2,128)S(1)} %broadcast_subtract_fusion), kind=kOutput, calls=%fused_computation.55 | convolution fusion | flops 541081600 | bytes 4358144 | tf_op jit(solution)/shard_map/fjp,fpc->cfj/dot_general | solution.py:134
  328.6 5.4 %collective-permute-start.3 = (bf16[128,128]{0,1:T(8,128)(2,1)S(1)}, bf16[128,128]{0,1:T(8,128)(2,1)S(1)}, u32[]{:S(2)}, u32[]{:S(2)}) collective-permute-start(bf16[128,128]{0,1:T(8,128)(2,1)S(1)} %bitcast.77), channel_id=1, source_target_pairs={{1,0},{2,1},{3,2},{4,3},{5,4},{6,5},{7,6},{8,7},{9,8},{10,9},{11,1... | collective-permute-start | bytes 98312 | tf_op jit(solution)/shard_map/ppermute | solution.py:23
  (213 shorter events, 64.8 us)
Async XLA Ops:
  7.2 69.1 %all-gather.5.cloned.1.call-start = ((), (), s32[]{:S(2)}) async-start(), calls=%async_computation.1 | async-start | bytes 10616832 | tf_op jit(solution)/shard_map/all_gather | solution.py:105
  76.3 112.9 %copy-start.3 = (bf16[11,256]{1,0:T(8,128)(2,1)S(1)}, bf16[11,256]{1,0:T(8,128)(2,1)}, u32[]{:S(2)}) copy-start(bf16[11,256]{1,0:T(8,128)(2,1)} %param.14) | copy-start | bytes 16900
  76.3 14.5 %collective-permute-start = (bf16[2,256,64]{1,2,0:T(8,128)(2,1)S(1)}, bf16[2,256,64]{1,2,0:T(8,128)(2,1)S(1)}, u32[]{:S(2)}, u32[]{:S(2)}) collective-permute-start(bf16[2,256,64]{1,2,0:T(8,128)(2,1)S(1)} %get-tuple-element.195), channel_id=1, source_target_pairs={{1,0},{2,1},{3,2},{4,3},{5,4},{6,5},{7,6},{8,7},{9,8},{10,9},{11,1... | collective-permute-start | bytes 196616 | tf_op jit(solution)/shard_map/while/body/eval_jaxpr/ppermute | solution.py:23
  82.6 8.3 %collective-permute-start.1 = (bf16[2,256,64]{1,2,0:T(8,128)(2,1)S(1)}, bf16[2,256,64]{1,2,0:T(8,128)(2,1)S(1)}, u32[]{:S(2)}, u32[]{:S(2)}) collective-permute-start(bf16[2,256,64]{1,2,0:T(8,128)(2,1)S(1)} %get-tuple-element.196), channel_id=1, source_target_pairs={{0,1},{1,2},{2,3},{3,4},{4,5},{5,6},{6,7},{7,8},{8,9},{9,10},{10,1... | collective-permute-start | bytes 196616 | tf_op jit(solution)/shard_map/while/body/eval_jaxpr/ppermute | solution.py:22
  94.2 10.2 %collective-permute-start = (bf16[2,256,64]{1,2,0:T(8,128)(2,1)S(1)}, bf16[2,256,64]{1,2,0:T(8,128)(2,1)S(1)}, u32[]{:S(2)}, u32[]{:S(2)}) collective-permute-start(bf16[2,256,64]{1,2,0:T(8,128)(2,1)S(1)} %get-tuple-element.195), channel_id=1, source_target_pairs={{1,0},{2,1},{3,2},{4,3},{5,4},{6,5},{7,6},{8,7},{9,8},{10,9},{11,1... | collective-permute-start | bytes 196616 | tf_op jit(solution)/shard_map/while/body/eval_jaxpr/ppermute | solution.py:23
  96.1 8.3 %collective-permute-start.1 = (bf16[2,256,64]{1,2,0:T(8,128)(2,1)S(1)}, bf16[2,256,64]{1,2,0:T(8,128)(2,1)S(1)}, u32[]{:S(2)}, u32[]{:S(2)}) collective-permute-start(bf16[2,256,64]{1,2,0:T(8,128)(2,1)S(1)} %get-tuple-element.196), channel_id=1, source_target_pairs={{0,1},{1,2},{2,3},{3,4},{4,5},{5,6},{6,7},{7,8},{8,9},{9,10},{10,1... | collective-permute-start | bytes 196616 | tf_op jit(solution)/shard_map/while/body/eval_jaxpr/ppermute | solution.py:22
  107.8 10.2 %collective-permute-start = (bf16[2,256,64]{1,2,0:T(8,128)(2,1)S(1)}, bf16[2,256,64]{1,2,0:T(8,128)(2,1)S(1)}, u32[]{:S(2)}, u32[]{:S(2)}) collective-permute-start(bf16[2,256,64]{1,2,0:T(8,128)(2,1)S(1)} %get-tuple-element.195), channel_id=1, source_target_pairs={{1,0},{2,1},{3,2},{4,3},{5,4},{6,5},{7,6},{8,7},{9,8},{10,9},{11,1... | collective-permute-start | bytes 196616 | tf_op jit(solution)/shard_map/while/body/eval_jaxpr/ppermute | solution.py:23
  109.7 8.3 %collective-permute-start.1 = (bf16[2,256,64]{1,2,0:T(8,128)(2,1)S(1)}, bf16[2,256,64]{1,2,0:T(8,128)(2,1)S(1)}, u32[]{:S(2)}, u32[]{:S(2)}) collective-permute-start(bf16[2,256,64]{1,2,0:T(8,128)(2,1)S(1)} %get-tuple-element.196), channel_id=1, source_target_pairs={{0,1},{1,2},{2,3},{3,4},{4,5},{5,6},{6,7},{7,8},{8,9},{9,10},{10,1... | collective-permute-start | bytes 196616 | tf_op jit(solution)/shard_map/while/body/eval_jaxpr/ppermute | solution.py:22
  121.3 10.2 %collective-permute-start = (bf16[2,256,64]{1,2,0:T(8,128)(2,1)S(1)}, bf16[2,256,64]{1,2,0:T(8,128)(2,1)S(1)}, u32[]{:S(2)}, u32[]{:S(2)}) collective-permute-start(bf16[2,256,64]{1,2,0:T(8,128)(2,1)S(1)} %get-tuple-element.195), channel_id=1, source_target_pairs={{1,0},{2,1},{3,2},{4,3},{5,4},{6,5},{7,6},{8,7},{9,8},{10,9},{11,1... | collective-permute-start | bytes 196616 | tf_op jit(solution)/shard_map/while/body/eval_jaxpr/ppermute | solution.py:23
  123.3 8.3 %collective-permute-start.1 = (bf16[2,256,64]{1,2,0:T(8,128)(2,1)S(1)}, bf16[2,256,64]{1,2,0:T(8,128)(2,1)S(1)}, u32[]{:S(2)}, u32[]{:S(2)}) collective-permute-start(bf16[2,256,64]{1,2,0:T(8,128)(2,1)S(1)} %get-tuple-element.196), channel_id=1, source_target_pairs={{0,1},{1,2},{2,3},{3,4},{4,5},{5,6},{6,7},{7,8},{8,9},{9,10},{10,1... | collective-permute-start | bytes 196616 | tf_op jit(solution)/shard_map/while/body/eval_jaxpr/ppermute | solution.py:22
  134.9 10.2 %collective-permute-start = (bf16[2,256,64]{1,2,0:T(8,128)(2,1)S(1)}, bf16[2,256,64]{1,2,0:T(8,128)(2,1)S(1)}, u32[]{:S(2)}, u32[]{:S(2)}) collective-permute-start(bf16[2,256,64]{1,2,0:T(8,128)(2,1)S(1)} %get-tuple-element.195), channel_id=1, source_target_pairs={{1,0},{2,1},{3,2},{4,3},{5,4},{6,5},{7,6},{8,7},{9,8},{10,9},{11,1... | collective-permute-start | bytes 196616 | tf_op jit(solution)/shard_map/while/body/eval_jaxpr/ppermute | solution.py:23
  136.8 8.3 %collective-permute-start.1 = (bf16[2,256,64]{1,2,0:T(8,128)(2,1)S(1)}, bf16[2,256,64]{1,2,0:T(8,128)(2,1)S(1)}, u32[]{:S(2)}, u32[]{:S(2)}) collective-permute-start(bf16[2,256,64]{1,2,0:T(8,128)(2,1)S(1)} %get-tuple-element.196), channel_id=1, source_target_pairs={{0,1},{1,2},{2,3},{3,4},{4,5},{5,6},{6,7},{7,8},{8,9},{9,10},{10,1... | collective-permute-start | bytes 196616 | tf_op jit(solution)/shard_map/while/body/eval_jaxpr/ppermute | solution.py:22
  148.5 10.2 %collective-permute-start = (bf16[2,256,64]{1,2,0:T(8,128)(2,1)S(1)}, bf16[2,256,64]{1,2,0:T(8,128)(2,1)S(1)}, u32[]{:S(2)}, u32[]{:S(2)}) collective-permute-start(bf16[2,256,64]{1,2,0:T(8,128)(2,1)S(1)} %get-tuple-element.195), channel_id=1, source_target_pairs={{1,0},{2,1},{3,2},{4,3},{5,4},{6,5},{7,6},{8,7},{9,8},{10,9},{11,1... | collective-permute-start | bytes 196616 | tf_op jit(solution)/shard_map/while/body/eval_jaxpr/ppermute | solution.py:23
  150.4 8.3 %collective-permute-start.1 = (bf16[2,256,64]{1,2,0:T(8,128)(2,1)S(1)}, bf16[2,256,64]{1,2,0:T(8,128)(2,1)S(1)}, u32[]{:S(2)}, u32[]{:S(2)}) collective-permute-start(bf16[2,256,64]{1,2,0:T(8,128)(2,1)S(1)} %get-tuple-element.196), channel_id=1, source_target_pairs={{0,1},{1,2},{2,3},{3,4},{4,5},{5,6},{6,7},{7,8},{8,9},{9,10},{10,1... | collective-permute-start | bytes 196616 | tf_op jit(solution)/shard_map/while/body/eval_jaxpr/ppermute | solution.py:22
  162.1 10.2 %collective-permute-start = (bf16[2,256,64]{1,2,0:T(8,128)(2,1)S(1)}, bf16[2,256,64]{1,2,0:T(8,128)(2,1)S(1)}, u32[]{:S(2)}, u32[]{:S(2)}) collective-permute-start(bf16[2,256,64]{1,2,0:T(8,128)(2,1)S(1)} %get-tuple-element.195), channel_id=1, source_target_pairs={{1,0},{2,1},{3,2},{4,3},{5,4},{6,5},{7,6},{8,7},{9,8},{10,9},{11,1... | collective-permute-start | bytes 196616 | tf_op jit(solution)/shard_map/while/body/eval_jaxpr/ppermute | solution.py:23
  164.0 8.3 %collective-permute-start.1 = (bf16[2,256,64]{1,2,0:T(8,128)(2,1)S(1)}, bf16[2,256,64]{1,2,0:T(8,128)(2,1)S(1)}, u32[]{:S(2)}, u32[]{:S(2)}) collective-permute-start(bf16[2,256,64]{1,2,0:T(8,128)(2,1)S(1)} %get-tuple-element.196), channel_id=1, source_target_pairs={{0,1},{1,2},{2,3},{3,4},{4,5},{5,6},{6,7},{7,8},{8,9},{9,10},{10,1... | collective-permute-start | bytes 196616 | tf_op jit(solution)/shard_map/while/body/eval_jaxpr/ppermute | solution.py:22
  175.6 10.2 %collective-permute-start = (bf16[2,256,64]{1,2,0:T(8,128)(2,1)S(1)}, bf16[2,256,64]{1,2,0:T(8,128)(2,1)S(1)}, u32[]{:S(2)}, u32[]{:S(2)}) collective-permute-start(bf16[2,256,64]{1,2,0:T(8,128)(2,1)S(1)} %get-tuple-element.195), channel_id=1, source_target_pairs={{1,0},{2,1},{3,2},{4,3},{5,4},{6,5},{7,6},{8,7},{9,8},{10,9},{11,1... | collective-permute-start | bytes 196616 | tf_op jit(solution)/shard_map/while/body/eval_jaxpr/ppermute | solution.py:23
  177.5 8.3 %collective-permute-start.1 = (bf16[2,256,64]{1,2,0:T(8,128)(2,1)S(1)}, bf16[2,256,64]{1,2,0:T(8,128)(2,1)S(1)}, u32[]{:S(2)}, u32[]{:S(2)}) collective-permute-start(bf16[2,256,64]{1,2,0:T(8,128)(2,1)S(1)} %get-tuple-element.196), channel_id=1, source_target_pairs={{0,1},{1,2},{2,3},{3,4},{4,5},{5,6},{6,7},{7,8},{8,9},{9,10},{10,1... | collective-permute-start | bytes 196616 | tf_op jit(solution)/shard_map/while/body/eval_jaxpr/ppermute | solution.py:22
  191.2 35.3 %all-to-all-start = ((bf16[64,2,11,256]{3,1,2,0:T(2,128)(2,1)}), bf16[64,2,11,256]{3,1,2,0:T(2,128)(2,1)S(1)}, u32[]{:S(2)}, u32[]{:S(2)}) async-start(bf16[64,2,11,256]{3,1,2,0:T(2,128)(2,1)} %broadcast_in_dim.201), calls=%async_computation | async-start | bytes 1441792 | tf_op jit(solution)/shard_map/all_to_all | solution.py:36
  196.7 122.6 %all-gather.7.cloned.1.call-start = ((), (), s32[]{:S(2)}) async-start(), calls=%async_computation.2 | async-start | bytes 4456448 | tf_op jit(solution)/shard_map/all_gather | solution.py:48
  287.4 48.7 %copy-start.1 = (bf16[576,384]{1,0:T(8,128)(2,1)S(1)}, bf16[576,384]{1,0:T(8,128)(2,1)}, u32[]{:S(2)}) copy-start(bf16[576,384]{1,0:T(8,128)(2,1)} %param.20) | copy-start | bytes 1327108
  287.4 48.7 %copy-start.2 = (bf16[384,20]{0,1:T(8,128)(2,1)S(1)}, bf16[384,20]{0,1:T(8,128)(2,1)}, u32[]{:S(2)}) copy-start(bf16[384,20]{0,1:T(8,128)(2,1)} %param.21) | copy-start | bytes 46084
  326.1 8.0 %collective-permute-start.2 = (bf16[128,128]{0,1:T(8,128)(2,1)S(1)}, bf16[128,128]{0,1:T(8,128)(2,1)S(1)}, u32[]{:S(2)}, u32[]{:S(2)}) collective-permute-start(bf16[128,128]{0,1:T(8,128)(2,1)S(1)} %bitcast.76), channel_id=1, source_target_pairs={{0,1},{1,2},{2,3},{3,4},{4,5},{5,6},{6,7},{7,8},{8,9},{9,10},{10,1... | collective-permute-start | bytes 98312 | tf_op jit(solution)/shard_map/ppermute | solution.py:22
  328.6 7.0 %collective-permute-start.3 = (bf16[128,128]{0,1:T(8,128)(2,1)S(1)}, bf16[128,128]{0,1:T(8,128)(2,1)S(1)}, u32[]{:S(2)}, u32[]{:S(2)}) collective-permute-start(bf16[128,128]{0,1:T(8,128)(2,1)S(1)} %bitcast.77), channel_id=1, source_target_pairs={{1,0},{2,1},{3,2},{4,3},{5,4},{6,5},{7,6},{8,7},{9,8},{10,9},{11,1... | collective-permute-start | bytes 98312 | tf_op jit(solution)/shard_map/ppermute | solution.py:23
  (6 other events, 79.2 us)
Sparse Core Ops, SparseCore 0:
  10.1 66.1 all-gather.4
  248.2 71.0 all-gather.6
where the time goes:
time: 345 us; the launch traced here: 344 us
  waiting for transfers between devices  168 us (49%)
  starting transfers between devices  62.5 us (18%)
  blocking collectives  52.2 us (15%)
  matrix products  31 us (9%)
  between operations  14.3 us (4%)
  other arithmetic  10.2 us (3%)
  local copies, waits for them, and re-layouts  4.91 us (1%)
    all_gather x1, waiting for transfers between devices, local(): weights = lax.all_gather(conv_weight, 'phase', axis=0, tiled=True)  67.4 us
    all_gather x3, blocking collectives, whole_of(): filled = lax.all_gather(filled, axes[number], axis=dim, tiled=True)  52.2 us
    ppermute x9, waiting for transfers between devices, padded_2(): before = lax.ppermute(last, axis, up)  36.4 us
    ppermute x9, starting transfers between devices, padded_2(): before = lax.ppermute(last, axis, up)  31.9 us
    all_gather x1, waiting for transfers between devices, whole_of(): filled = lax.all_gather(filled, axes[number], axis=dim, tiled=True)  31.9 us
    all_to_all x1, waiting for transfers between devices, copy_for_each(): lax.all_to_all(jnp.broadcast_to(value[None], (devices, *value.shape)), ax...  29.8 us
    ppermute x9, starting transfers between devices, padded_2(): after = lax.ppermute(first, axis, down)  25.1 us
    dot_general x8, matrix products, image_layer(): jnp.einsum('ok,fkp->fop', weight, stacked, preferred_element_type=jnp.flo...  16.7 us
  transfers between devices with their start and end apart: 21, of which 12 were waited for; matrix products, arithmetic and copies ran while one was open for 0% of the time, Pallas kernels for 0%

commit v1 on v0

v1 whole, which is shorter than its diff:
```python
import functools

import jax
import jax.numpy as jnp
from jax import lax
from jax.experimental import pallas as pl
from jax.experimental.pallas import tpu as pltpu
from jax.sharding import PartitionSpec as P

C = 256
ROWS = 24
CHUNK = 8
M = CHUNK * 64
BUF = 1792
MESH = pl.DeviceIdType.MESH


def layers(act, weights, first_layer, last_layer, top_row):
    column = lax.broadcasted_iota(jnp.int32, (M, 1), 0) % 64
    has_left = column >= 1
    has_right = column < 63
    row_in_chunk = lax.broadcasted_iota(jnp.int32, (M, 1), 0) // 64

    def layer(number, carry):
        now, later = number % 2, (number + 1) % 2

        def chunk(step, inner):
            start = pl.multiple_of((number + 1) * 64 + step * M, 64)
            centre = act[now, pl.ds(start, M), :]
            lhs = jnp.concatenate(
                [act[now, pl.ds(start - 64, M), :], centre, act[now, pl.ds(start + 64, M), :]], axis=1
            )

            def part(tap):
                rhs = jnp.concatenate(
                    [weights[number, :, (3 * r + tap) * C : (3 * r + tap + 1) * C] for r in range(3)], axis=1
                )
                return lax.dot_general(
                    lhs, rhs, (((1,), (1,)), ((), ())), preferred_element_type=jnp.float32
                )

            total = part(1)
            total = total + jnp.where(has_left, pltpu.roll(part(0), 1, 0), 0.0)
            total = total + jnp.where(has_right, pltpu.roll(part(2), M - 1, 0), 0.0)
            row = top_row + start // 64 + row_in_chunk
            new = centre.astype(jnp.float32) + jnp.maximum(total, 0.0)
            new = jnp.where((row >= 0) & (row < 256), new, 0.0)
            act[later, pl.ds(start, M), :] = new.astype(jnp.bfloat16)
            return inner

        lax.fori_loop(0, (22 - 2 * number + CHUNK - 1) // CHUNK, chunk, 0)
        return carry

    lax.fori_loop(first_layer, last_layer, layer, 0)


def image_kernel(
    img, w_own, cwq, pts, sc, table, points, weights, act,
    own_sem, send_sem, h_sem, y1_sem, y2_sem, x1_sem, x2_sem, d_sem, tz_sem, tx_sem, pz_sem, px_sem, s_sem, ag_send,
):
    p = lax.axis_index("phase")
    w = lax.axis_index("wide")
    y, c = p // 2, p % 2
    x, z = w // 16, w % 16
    k, t = w // 2, w % 2
    top_row = 8 * k - 8

    def at(phase, wide):
        return {"phase": phase, "wide": wide}

    def y_dev(step):
        return at(2 * ((y + step + 4) % 4) + c, w)

    def x_dev(step):
        return at(p, 16 * ((x + step + 4) % 4) + z)

    def z_dev(step):
        return at(p, 16 * x + (z + step) % 16)

    partner = at(2 * y + 1 - c, w)
    sibling = at(p, 2 * k + 1 - t)
    halo_peers = [(d, f) for d in (-1, 1) for f in (0, 1)]

    own_copy = pltpu.make_async_copy(w_own.at[0], weights.at[p], own_sem)
    own_copy.start()
    barrier = pltpu.get_barrier_semaphore()
    peers = [y_dev(1), y_dev(-1), partner, sibling]
    peers += [x_dev(e) for e in (1, 2, 3)] + [z_dev(d) for d in range(1, 16)]
    peers += [at(p, (2 * (k + d) + f + 64) % 64) for d, f in halo_peers]
    for peer in peers:
        pl.semaphore_signal(barrier, inc=1, device_id=peer, device_id_type=MESH)
    pl.semaphore_wait(barrier, len(peers))

    sends = []

    def send(src, dst, recv, device):
        number = len(sends)
        copy = pltpu.make_async_remote_copy(
            src_ref=src, dst_ref=dst, send_sem=send_sem.at[number], recv_sem=recv,
            device_id=device, device_id_type=MESH,
        )
        copy.start()
        sends.append(copy)

    def arrived(ref, recv):
        pltpu.make_async_remote_copy(
            src_ref=ref, dst_ref=ref, send_sem=send_sem.at[0], recv_sem=recv,
            device_id=partner, device_id_type=MESH,
        ).wait_recv()

    def block(j):
        return act.at[0, pl.ds(pl.multiple_of(j * 256, 256), 256), :]

    send(img.at[1 - t], block(2 + t), h_sem.at[2 + t], sibling)
    for d, f in halo_peers:
        send(img.at[f], block(2 - 2 * d + t), h_sem.at[2 - 2 * d + t], at(p, (2 * (k + d) + f + 64) % 64))

    def q_cols(layer, owner, first=0, tiles=3):
        return weights.at[layer, :, pl.ds(pl.multiple_of(768 + 384 * owner + 128 * first, 128), 128 * tiles)]

    def a_cols(layer, first=0, tiles=6):
        return weights.at[layer, :, pl.ds(128 * first, 128 * tiles)]

    def layer_of(step):
        return 2 * ((y + step + 8) % 4) + c

    sign = 1 - 2 * c
    own_copy.wait()
    for d in range(2):
        step = sign * (1 - 2 * d)
        send(q_cols(p, x), q_cols(p, x), y1_sem.at[d, 0], y_dev(step))
    for d in range(2):
        step = sign * (1 - 2 * d)
        send(a_cols(p), a_cols(p), y1_sem.at[d, 1], y_dev(step))
    send(weights.at[p], weights.at[p], d_sem.at[3], partner)

    q_parts = ((0, 2), (2, 1))
    a_parts = ((0, 3), (3, 3))
    near = [layer_of(-sign), layer_of(sign)]
    far = layer_of(2)

    def x_first(layer, j):
        for d in range(2):
            send(q_cols(layer, x), q_cols(layer, x), x1_sem.at[d, j], x_dev(sign * (1 - 2 * d)))

    def x_second(layer, j):
        for d in range(2):
            step = sign * (1 - 2 * d)
            source = (x - step + 4) % 4
            arrived(q_cols(layer, source), x1_sem.at[d, j])
            part = q_cols(layer, source, *q_parts[d])
            send(part, part, x2_sem.at[d, j], x_dev(step))

    def x_done(layer, j):
        for d in range(2):
            arrived(q_cols(layer, (x + 2) % 4, *q_parts[d]), x2_sem.at[d, j])

    for d in range(2):
        step = sign * (1 - 2 * d)
        arrived(q_cols(near[d], x), y1_sem.at[d, 0])
        part = q_cols(near[d], x, *q_parts[d])
        send(part, part, y2_sem.at[d, 0], y_dev(step))
    for d in range(2):
        x_first(near[d], d)
    for d in range(2):
        step = sign * (1 - 2 * d)
        arrived(a_cols(near[d]), y1_sem.at[d, 1])
        part = a_cols(near[d], *a_parts[d])
        send(part, part, y2_sem.at[d, 1], y_dev(step))
    for d in range(2):
        arrived(q_cols(far, x, *q_parts[d]), y2_sem.at[d, 0])
    x_first(far, 2)
    for d in range(2):
        x_second(near[d], d)
    for d in range(2):
        x_done(near[d], d)
        send(weights.at[near[d]], weights.at[near[d]], d_sem.at[d], partner)
    x_second(far, 2)
    for d in range(2):
        arrived(a_cols(far, *a_parts[d]), y2_sem.at[d, 1])
    x_done(far, 2)
    send(weights.at[far], weights.at[far], d_sem.at[2], partner)

    order = (8, 7, 9, 6, 10, 5, 11, 4, 12, 3, 13, 2, 14, 1, 15)

    def spread_z(ref, sem, number):
        own = ref.at[w]
        for d in order:
            pltpu.make_async_remote_copy(
                src_ref=own, dst_ref=own, send_sem=ag_send.at[number], recv_sem=sem.at[d],
                device_id=z_dev(d), device_id_type=MESH,
            ).start()

    def forward(ref, sem, source, number):
        for e in (1, 2, 3):
            pltpu.make_async_remote_copy(
                src_ref=ref.at[source], dst_ref=ref.at[source], send_sem=ag_send.at[number], recv_sem=sem.at[e],
                device_id=x_dev(e), device_id_type=MESH,
            ).start()

    def spread_x(ref, z_sem, x_sem, number):
        forward(ref, x_sem, w, number)
        for d in reversed(order):
            source = 16 * x + (z - d + 16) % 16
            arrived(ref.at[source], z_sem.at[d])
            forward(ref, x_sem, source, number)

    def spread_end(ref, x_sem, number):
        for e in (1, 2, 3):
            arrived(ref.at[pl.ds(16 * ((x - e + 4) % 4), 16)], x_sem.at[e])
        pltpu.make_async_remote_copy(
            src_ref=ref.at[pl.ds(0, 63)], dst_ref=ref.at[pl.ds(0, 63)], send_sem=ag_send.at[number],
            recv_sem=own_sem, device_id=partner, device_id_type=MESH,
        ).wait_send()

    points[w] = pts[...]
    spread_z(points, pz_sem, 0)

    act[0, pl.ds(pl.multiple_of((2 + t) * 256, 256), 256), :] = img[t]
    for j in (0, 1, 4, 5):
        arrived(block(j), h_sem.at[j])
    arrived(block(3 - t), h_sem.at[3 - t])

    @pl.when(k == 0)
    def _():
        act[0, pl.ds(0, 512), :] = jnp.zeros((512, C), jnp.bfloat16)

    @pl.when(k == 31)
    def _():
        act[0, pl.ds(1024, 512), :] = jnp.zeros((512, C), jnp.bfloat16)

    other = 1 - c
    their_sign = 1 - 2 * other
    theirs = [2 * ((y - their_sign + 4) % 4) + other, 2 * ((y + their_sign + 4) % 4) + other,
              2 * ((y + 2) % 4) + other, 2 * y + other]
    for j in (3, 0, 1, 2):
        arrived(weights.at[theirs[j]], d_sem.at[j])

    layers(act, weights, 0, 4, top_row)
    spread_x(points, pz_sem, px_sem, 0)
    layers(act, weights, 4, 8, top_row)

    total = None
    for q in range(4):
        part = lax.dot_general(
            cwq[q], act[0, pl.ds(512 + 128 * q, 128), :], (((1,), (1,)), ((), ())),
            preferred_element_type=jnp.float32,
        )
        total = part if total is None else total + part
    table[w] = total.astype(jnp.bfloat16)
    sc[t] = total
    spread_z(table, tz_sem, 1)
    send(sc.at[t], sc.at[t], s_sem, sibling)
    spread_x(table, tz_sem, tx_sem, 1)
    spread_end(points, px_sem, 0)
    spread_end(table, tx_sem, 1)
    arrived(sc.at[1 - t], s_sem)
    for copy in sends:
        copy.wait_send()


N_SENDS = 48


def image_part(img, conv_weight, cwq, pts):
    vmem = pl.BlockSpec(memory_space=pltpu.VMEM)
    dma = pltpu.SemaphoreType.DMA
    return pl.pallas_call(
        image_kernel,
        name="image_part",
        out_shape=(
            jax.ShapeDtypeStruct((2, 48, 128), jnp.float32),
            jax.ShapeDtypeStruct((64, 48, 128), jnp.bfloat16),
            jax.ShapeDtypeStruct((64, 32, 128), jnp.float32),
        ),
        in_specs=[vmem, pl.BlockSpec(memory_space=pl.ANY), vmem, vmem],
        out_specs=(vmem, vmem, vmem),
        scratch_shapes=[
            pltpu.VMEM((8, C, 9 * C), jnp.bfloat16),
            pltpu.VMEM((2, BUF, C), jnp.bfloat16),
            dma, dma((N_SENDS,)), dma((6,)), dma((2, 2)), dma((2, 2)), dma((2, 3)), dma((2, 3)), dma((4,)),
            dma((16,)), dma((4,)), dma((16,)), dma((4,)), dma, dma((2,)),
        ],
        compiler_params=pltpu.CompilerParams(
            collective_id=0, has_side_effects=True, vmem_limit_bytes=40 * 2**20
        ),
        cost_estimate=pl.CostEstimate(flops=10**10, bytes_accessed=10**7, transcendentals=0),
    )(img, conv_weight, cwq, pts)


SLOTS = 128
GROUP = 16
LANES = 256


def point_kernel(points, table, wk, bev, head, out, place, packed, pooled):
    w = lax.axis_index("wide")
    first_cell = ((w - 1) * 128).astype(jnp.float32)
    one, zero = jnp.float32(1.0), jnp.float32(0.0)

    def iota(shape, dim):
        return lax.broadcasted_iota(jnp.int32, shape, dim).astype(jnp.float32)

    def where_bf16(mask):
        return jnp.where(mask, one, zero).astype(jnp.bfloat16)

    def split(value):
        high = value.astype(jnp.bfloat16)
        return high, (value - high.astype(jnp.float32)).astype(jnp.bfloat16)

    row_i = lax.broadcasted_iota(jnp.int32, (128, 128), 0)
    col_i = lax.broadcasted_iota(jnp.int32, (128, 128), 1)
    up_to = where_bf16(row_i <= col_i)
    row_j = lax.broadcasted_iota(jnp.int32, (64, 64), 0)
    col_j = lax.broadcasted_iota(jnp.int32, (64, 64), 1)
    before = where_bf16((row_j // GROUP == col_j // GROUP) & (col_j < row_j))
    all_ones = jnp.ones((128, 128), jnp.bfloat16)
    slot_row = iota((SLOTS, 128), 0)
    low_row = iota((128, LANES), 0)
    quarter_row = lax.broadcasted_iota(jnp.int32, (48, LANES), 0) // 11
    quarter_row = quarter_row.astype(jnp.float32)
    class_i = lax.broadcasted_iota(jnp.int32, (16, 48), 0)
    class_j = lax.broadcasted_iota(jnp.int32, (16, 48), 1)
    to_class = where_bf16((class_j % 11 == class_i) & (class_j < 44))
    wk_high, wk_low = split(wk[...])
    wk_both = jnp.concatenate([wk_high, wk_low], axis=0)
    column = lax.broadcasted_iota(jnp.int32, (128, 1), 0)

    def frame(f, carry):
        most = zero
        for h in range(2):
            cell = points[pl.ds((2 * f + h) * 8 + 5, 64, stride=32), :] - first_cell
            mine = (cell >= 0.0) & (cell < 384.0)
            mine_16 = where_bf16(mine)
            inside = jnp.dot(mine_16, up_to, preferred_element_type=jnp.float32)
            row_sum = jnp.dot(mine_16, all_ones, preferred_element_type=jnp.float32)
            ahead = jnp.dot(before, row_sum.astype(jnp.bfloat16), preferred_element_type=jnp.float32)
            place[h] = jnp.where(mine, inside - 1.0 + ahead, -1.0)
            most = jnp.maximum(most, jnp.max(row_sum + ahead))
        passes = (most.astype(jnp.int32) + SLOTS - 1) // SLOTS
        pooled[...] = jnp.zeros_like(pooled)

        def one_pass(number, inner):
            slot = slot_row + (number * SLOTS).astype(jnp.float32)

            def group(g, state):
                h, first = g // 4, pl.multiple_of(g % 4 * GROUP, GROUP)
                places = place[h, pl.ds(first, GROUP), :]
                data, picks = [], []
                for i in range(GROUP):
                    rows = points[pl.ds(pl.multiple_of((first + i) * 32 + (2 * f + h) * 8, 8), 8), :]
                    high, low = split(rows)
                    data.append(jnp.concatenate([high.astype(jnp.float32), low.astype(jnp.float32)], axis=0))
                    picks.append(where_bf16(slot == places[i : i + 1, :]))
                chosen = lax.dot_general(
                    jnp.concatenate(data, axis=1).astype(jnp.bfloat16), jnp.concatenate(picks, axis=1),
                    (((1,), (1,)), ((), ())), preferred_element_type=jnp.float32,
                )
                packed[g] = chosen
                return state

            lax.fori_loop(0, 8, group, 0)

            def lanes(s, state):
                chosen = jnp.concatenate([packed[2 * s], packed[2 * s + 1]], axis=1)
                value = chosen[:8] + chosen[8:]
                pixel, cell, used = value[4:5], value[5:6] - first_cell, value[6:7]
                block = jnp.floor(pixel * (1.0 / 128.0))
                low = pixel - 128.0 * block
                pair = jnp.floor(block * 0.25)
                quarter = block - 4.0 * pair
                of_frame = jnp.concatenate([table[2 * i + f] for i in range(32)], axis=0)
                read = jnp.dot(of_frame, where_bf16(low_row == low), preferred_element_type=jnp.float32)
                total = jnp.zeros((48, LANES), jnp.float32)
                for i in range(32):
                    total = total + jnp.where(pair == float(i), read[48 * i : 48 * i + 48], 0.0)
                total = jnp.where(quarter_row == quarter, total, 0.0)
                painted = jnp.dot(to_class, total.astype(jnp.bfloat16), preferred_element_type=jnp.float32)
                gate = jax.nn.sigmoid(painted)
                gate_high, gate_low = split(gate)
                features = jnp.concatenate([chosen.astype(jnp.bfloat16), gate_high, gate_low], axis=0)
                both = jnp.dot(wk_both, features, preferred_element_type=jnp.float32)
                hidden = jnp.maximum(both[:64] + both[64:], 0.0)
                row = jnp.floor(cell * (1.0 / 128.0))
                col = cell - 128.0 * row
                row = jnp.where(used > 0.5, row, -1.0)
                by_row = jnp.concatenate(
                    [jnp.where(row == float(r), hidden, 0.0) for r in range(3)], axis=0
                ).astype(jnp.bfloat16)
                pooled[...] += lax.dot_general(
                    where_bf16(low_row == col), by_row, (((1,), (1,)), ((), ())),
                    preferred_element_type=jnp.float32,
                )
                return state

            lax.fori_loop(0, 8 * SLOTS // LANES, lanes, 0)
            return inner

        lax.fori_loop(0, passes, one_pass, 0)
        grid = pooled[...]
        total = None
        for d in range(3):
            if d == 0:
                moved = jnp.where(column >= 1, pltpu.roll(grid, 1, 0), 0.0)
            elif d == 2:
                moved = jnp.where(column < 127, pltpu.roll(grid, 127, 0), 0.0)
            else:
                moved = grid
            weight = jnp.concatenate([bev[(3 * r + d) * 64 : (3 * r + d + 1) * 64, :] for r in range(3)], axis=0)
            part = jnp.dot(moved.astype(jnp.bfloat16), weight, preferred_element_type=jnp.float32)
            total = part if total is None else total + part
        feature = jnp.maximum(total, 0.0).astype(jnp.bfloat16)
        out[f] = jnp.dot(feature, head[...], preferred_element_type=jnp.float32)
        return carry

    lax.fori_loop(0, 2, frame, 0)


def point_part(points, table, wk, bev, head):
    vmem = pl.BlockSpec(memory_space=pltpu.VMEM)
    return pl.pallas_call(
        point_kernel,
        name="point_part",
        out_shape=jax.ShapeDtypeStruct((2, 128, 20), jnp.float32),
        in_specs=[vmem] * 5,
        out_specs=vmem,
        scratch_shapes=[
            pltpu.VMEM((2, 64, 128), jnp.float32),
            pltpu.VMEM((8, 16, SLOTS), jnp.float32),
            pltpu.VMEM((128, 192), jnp.float32),
        ],
        compiler_params=pltpu.CompilerParams(vmem_limit_bytes=40 * 2**20),
        cost_estimate=pl.CostEstimate(flops=10**9, bytes_accessed=3 * 10**6, transcendentals=10**5),
    )(points, table, wk, bev, head)


def local(
    image,
    conv_weight,
    class_weight,
    point_feats,
    pixel_index,
    pillar_index,
    point_counts,
    pillar_weight,
    bev_weight,
    head_weight,
):
    p = lax.axis_index("phase")
    t = lax.axis_index("wide") % 2
    img = jnp.swapaxes(lax.dynamic_slice_in_dim(image, 2 * p, 2, 0), 1, 2)
    live = jnp.arange(256, dtype=jnp.int32)[None, :] < point_counts
    cell = jnp.where(live, pillar_index, -1024)
    used = jnp.ones((2, 1, 256), jnp.float32)
    rows = [point_feats, pixel_index[:, None].astype(jnp.float32), cell[:, None].astype(jnp.float32), used, used]
    pts = jnp.concatenate(rows, axis=1).reshape(2, 8, 2, 128).transpose(0, 2, 1, 3).reshape(32, 128)
    cwq = jnp.stack([jnp.pad(class_weight, ((11 * q, 37 - 11 * q), (0, 0))) for q in range(4)])
    sc, table, points = image_part(img, conv_weight, cwq, pts)
    own = lax.dynamic_slice_in_dim(sc[:, :44].reshape(2, 4, 11, 128), 2 * t, 2, 1)
    scores = own.transpose(0, 2, 1, 3).reshape(2, 11, 256)
    raw, gates = pillar_weight[:, :4], jnp.pad(pillar_weight[:, 4:], ((0, 0), (0, 5)))
    raw = jnp.pad(raw, ((0, 0), (0, 4)))
    wk = jnp.concatenate([raw, raw, gates, gates], axis=1)
    detections = point_part(points.reshape(64 * 32, 128), table, wk, bev_weight, head_weight)
    return (detections, scores)


def solution(mesh):
    placed = (
        P(None, None, "wide"),
        P("phase", None, None),
        P(),
        P("phase", None, "wide"),
        P("phase", "wide"),
        P("phase", "wide"),
        P("phase", "wide"),
        P(),
        P(),
        P(),
    )
    return jax.shard_map(
        local,
        mesh=mesh,
        in_specs=placed,
        out_specs=(P("phase", "wide", None), P("phase", None, "wide")),
        check_vma=False,
    )
```

time: 345 us -> 115 us (0.33)
  the two profiles are of different devices: /device:TPU:6 before, /device:TPU:1 now
where the time goes in v1:
time: 115 us; the launch traced here: 114 us
  Pallas kernels  102 us (89%)
  local copies, waits for them, and re-layouts  9.08 us (8%)
  other arithmetic  2.32 us (2%)
    pallas_call x1, Pallas kernels, image_part(): pl.pallas_call(image_kernel, name='image_part', out_shape=(jax.ShapeDtype...  88.8 us
    pallas_call x1, Pallas kernels, point_part(): pl.pallas_call(point_kernel, name='point_part', out_shape=jax.ShapeDtypeS...  13.3 us
    unnamed x24, local copies, waits for them, and re-layouts  7.3 us

profile of v1, /device:TPU:1, one launch (start us, length us, event | category | flops | bytes accessed | tf_op | source)
XLA Modules:
  0.0 114.3 jit_solution(11721982391993213689)
XLA Ops:
  0.6 0.0 copy-start
  0.7 0.9 pad_bitcast_fusion.3
  1.6 0.7 copy-done
  2.3 0.1 copy.40
  2.5 0.7 convert_element_type.20
  3.2 0.8 fusion
  3.9 0.1 pad.37.clone
  4.0 0.8 maximum_maximum_fusion
  4.8 1.3 %copy-done.1 = bf16[1,256,2304]{2,1,0:T(8,128)(2,1)S(1)} copy-done((bf16[1,256,2304]{2,1,0:T(8,128)(2,1)S(1)}, bf16[1,256,2304]{2,1,0:T(8,128)(2,1)}, u32[]{:S(2)}) %copy-start.1) | copy-done | bytes 1179672
  6.1 0.0 copy-start.2
  6.1 88.8 %image_part.1 = (f32[2,48,128]{2,1,0:T(8,128)S(1)}, bf16[64,48,128]{2,1,0:T(8,128)(2,1)S(1)}, f32[64,32,128]{2,1,0:T(8,128)S(1)}) custom-call(bf16[2,256,256]{2,1,0:T(8,128)(2,1)S(1)} %bitcast.25, bf16[1,256,2304]{2,1,0:T(8,128)(2,1)S(1)} %copy-done.1, bf16[4,48,256]{2,1,0:T(8,128)(2,1)S(1)} %pad_maximum_fusion.cwq, f32[32,128]{1,0:T(8,128)S(1)} %bitcast.27), custom_call_target="tpu_custom_call" | custom-call | flops 10000000000 | bytes 10000000 | tf_op jit(solution)/shard_map/image_part/pallas_call | solution.py:268
  94.9 1.0 copy-done.3
  95.9 0.9 copy-done.5
  96.8 0.6 copy_bitcast_fusion
  97.5 0.1 copy.41
  97.6 0.1 copy.34
  97.7 0.1 pad_maximum_fusion.1.wk
  97.8 0.1 copy.36.head
  97.9 0.0 copy-done.2
  97.9 0.0 copy-start.4
  98.0 1.2 %copy-done.4 = f32[64,32,128]{2,1,0:T(8,128)S(1)} copy-done((f32[64,32,128]{2,1,0:T(8,128)S(1)}, f32[64,32,128]{2,1,0:T(8,128)}, u32[]{:S(2)}) %copy-start.4) | copy-done | bytes 1048600
  99.2 1.1 copy-done.6
  100.3 13.3 %point_part.1 = f32[2,128,20]{2,1,0:T(8,128)S(1)} custom-call(f32[2048,128]{1,0:T(8,128)S(1)} %bitcast.28, bf16[64,48,128]{2,1,0:T(8,128)(2,1)S(1)} %copy-done.6, f32[64,48]{1,0:T(8,128)S(1)} %pad_maximum_fusion.1.wk, bf16[576,384]{1,0:T(8,128)(2,1)S(1)} %copy-done.2, bf16[384,20]{1,0:T(8,128)(2,1)S(1)} %copy.36.head), custom_call_target="tpu_custom_call" | custom-call | flops 1000000000 | bytes 3000000 | tf_op jit(solution)/shard_map/point_part/pallas_call | solution.py:421
  113.6 0.7 copy.39
  (21 shorter events, 0.1 us)
Async XLA Ops:
  0.6 1.7 %copy-start = (bf16[16,256,256]{2,1,0:T(8,128)(2,1)S(1)}, bf16[16,256,256]{2,1,0:T(8,128)(2,1)}, u32[]{:S(2)}) copy-start(bf16[16,256,256]{2,1,0:T(8,128)(2,1)} %param.10) | copy-start | bytes 6291460
  4.8 1.3 %copy-start.1 = (bf16[1,256,2304]{2,1,0:T(8,128)(2,1)S(1)}, bf16[1,256,2304]{2,1,0:T(8,128)(2,1)}, u32[]{:S(2)}) copy-start(bf16[1,256,2304]{2,1,0:T(8,128)(2,1)} %w_own.1) | copy-start | bytes 3538948
  6.0 91.4 %copy-start.8 = (f32[64,15]{0,1:T(8,128)S(1)}, f32[64,15]{0,1:T(8,128)}, u32[]{:S(2)}) copy-start(f32[64,15]{0,1:T(8,128)} %param.17) | copy-start | bytes 11524
  6.0 91.5 %slice-start = ((f32[64,15]{0,1:T(8,128)}), f32[64,8]{0,1:T(8,128)S(1)}, s32[]{:S(2)}) async-start(f32[64,15]{0,1:T(8,128)} %param.17), calls=%async_computation | async-start | bytes 8192 | tf_op jit(solution)/shard_map/slice
  6.0 91.6 %copy-start.9 = (pred[8]{0:T(512)(128)(4,1)S(1)}, pred[8]{0:T(512)(128)(4,1)}, u32[]{:S(2)}) copy-start(pred[8]{0:T(512)(128)(4,1)} %constant.32.clone.1) | copy-start | bytes 28
  6.0 91.7 %copy-start.7 = (bf16[384,20]{0,1:T(8,128)(2,1)S(1)}, bf16[384,20]{0,1:T(8,128)(2,1)}, u32[]{:S(2)}) copy-start(bf16[384,20]{0,1:T(8,128)(2,1)} %param.19) | copy-start | bytes 46084
  6.1 91.9 %copy-start.2 = (bf16[576,384]{1,0:T(8,128)(2,1)S(1)}, bf16[576,384]{1,0:T(8,128)(2,1)}, u32[]{:S(2)}) copy-start(bf16[576,384]{1,0:T(8,128)(2,1)} %bev.1) | copy-start | bytes 1327108
  94.9 1.0 copy-start.3
  95.9 0.9 copy-start.5
  97.9 1.2 %copy-start.4 = (f32[64,32,128]{2,1,0:T(8,128)S(1)}, f32[64,32,128]{2,1,0:T(8,128)}, u32[]{:S(2)}) copy-start(f32[64,32,128]{2,1,0:T(8,128)} %copy-done.3) | copy-start | bytes 3145732
  99.2 1.1 copy-start.6

commit v2 on v1

--- a/solution.py
+++ b/solution.py
@@ -9,54 +9,43 @@
 
 C = 256
 ROWS = 24
-CHUNK = 8
-M = CHUNK * 64
-BUF = 1792
+MOST_ROWS = 12
 MESH = pl.DeviceIdType.MESH
-
-
-def layers(act, weights, first_layer, last_layer, top_row):
-    column = lax.broadcasted_iota(jnp.int32, (M, 1), 0) % 64
-    has_left = column >= 1
-    has_right = column < 63
-    row_in_chunk = lax.broadcasted_iota(jnp.int32, (M, 1), 0) // 64
-
-    def layer(number, carry):
+NEAR = (4, -4, 3, -3, 2, -2, 1, -1)
+EARLY = (0, 4, -4, 1, -1, 2, -2, 3, -3)
+LATE = (5, -5, 6, -6, 7, -7, 8)
+
+
+def layers(act, weights, numbers, top_row):
+    for number in numbers:
         now, later = number % 2, (number + 1) % 2
-
-        def chunk(step, inner):
-            start = pl.multiple_of((number + 1) * 64 + step * M, 64)
-            centre = act[now, pl.ds(start, M), :]
-            lhs = jnp.concatenate(
-                [act[now, pl.ds(start - 64, M), :], centre, act[now, pl.ds(start + 64, M), :]], axis=1
-            )
+        rows = 22 - 2 * number
+        half = rows if rows <= MOST_ROWS else (rows + 1) // 2
+        for first in range(0, rows, half):
+            count = min(half, rows - first) * 64
+            start = (number + 1 + first) * 64
+            column = lax.broadcasted_iota(jnp.int32, (count, 1), 0) % 64
+            row = lax.broadcasted_iota(jnp.int32, (count, 1), 0) // 64 + (top_row + number + 1 + first)
+            lhs = jnp.concatenate([act[now, pl.ds(start + 64 * r, count), :] for r in (-1, 0, 1)], axis=1)
 
             def part(tap):
                 rhs = jnp.concatenate(
                     [weights[number, :, (3 * r + tap) * C : (3 * r + tap + 1) * C] for r in range(3)], axis=1
                 )
-                return lax.dot_general(
-                    lhs, rhs, (((1,), (1,)), ((), ())), preferred_element_type=jnp.float32
-                )
+                return lax.dot_general(lhs, rhs, (((1,), (1,)), ((), ())), preferred_element_type=jnp.float32)
 
             total = part(1)
-            total = total + jnp.where(has_left, pltpu.roll(part(0), 1, 0), 0.0)
-            total = total + jnp.where(has_right, pltpu.roll(part(2), M - 1, 0), 0.0)
-            row = top_row + start // 64 + row_in_chunk
-            new = centre.astype(jnp.float32) + jnp.maximum(total, 0.0)
+            total = total + jnp.where(column >= 1, pltpu.roll(part(0), 1, 0), 0.0)
+            total = total + jnp.where(column < 63, pltpu.roll(part(2), count - 1, 0), 0.0)
+            new = act[now, pl.ds(start, count), :].astype(jnp.float32) + jnp.maximum(total, 0.0)
             new = jnp.where((row >= 0) & (row < 256), new, 0.0)
-            act[later, pl.ds(start, M), :] = new.astype(jnp.bfloat16)
-            return inner
-
-        lax.fori_loop(0, (22 - 2 * number + CHUNK - 1) // CHUNK, chunk, 0)
-        return carry
-
-    lax.fori_loop(first_layer, last_layer, layer, 0)
+            act[later, pl.ds(start, count), :] = new.astype(jnp.bfloat16)
 
 
 def image_kernel(
-    img, w_own, cwq, pts, sc, table, points, weights, act,
-    own_sem, send_sem, h_sem, y1_sem, y2_sem, x1_sem, x2_sem, d_sem, tz_sem, tx_sem, pz_sem, px_sem, s_sem, ag_send,
+    image, w_own, class_weight, feats, pixel, pillar, counts, sc, table, points, weights, act, raw, img,
+    own_sem, raw_sem, send_sem, h_sem, y1_sem, y2_sem, x1_sem, x2_sem, d_sem, tz_sem, tx_sem, tf_sem,
+    pz_sem, px_sem, pf_sem, s_sem, ag_send,
 ):
     p = lax.axis_index("phase")
     w = lax.axis_index("wide")
@@ -75,20 +64,35 @@
         return at(p, 16 * ((x + step + 4) % 4) + z)
 
     def z_dev(step):
-        return at(p, 16 * x + (z + step) % 16)
+        return at(p, 16 * x + (z + step + 16) % 16)
 
     partner = at(2 * y + 1 - c, w)
     sibling = at(p, 2 * k + 1 - t)
     halo_peers = [(d, f) for d in (-1, 1) for f in (0, 1)]
 
+    raw_copy = pltpu.make_async_copy(image.at[pl.ds(2 * p, 2)], raw, raw_sem)
+    raw_copy.start()
     own_copy = pltpu.make_async_copy(w_own.at[0], weights.at[p], own_sem)
     own_copy.start()
     barrier = pltpu.get_barrier_semaphore()
     peers = [y_dev(1), y_dev(-1), partner, sibling]
-    peers += [x_dev(e) for e in (1, 2, 3)] + [z_dev(d) for d in range(1, 16)]
+    peers += [x_dev(1), x_dev(-1)] + [z_dev(d) for d in NEAR]
     peers += [at(p, (2 * (k + d) + f + 64) % 64) for d, f in halo_peers]
     for peer in peers:
         pl.semaphore_signal(barrier, inc=1, device_id=peer, device_id_type=MESH)
+    lane = lax.broadcasted_iota(jnp.int32, (1, 256), 1)
+    for f in range(2):
+        cell = jnp.where(lane < counts[f : f + 1, :], pillar[f : f + 1, :], -1024).astype(jnp.float32)
+        where = pixel[f : f + 1, :].astype(jnp.float32)
+        for h in range(2):
+            first = (2 * f + h) * 8
+            points[w, first : first + 4, :] = feats[f, :, 128 * h : 128 * h + 128]
+            points[w, first + 4 : first + 5, :] = where[:, 128 * h : 128 * h + 128]
+            points[w, first + 5 : first + 6, :] = cell[:, 128 * h : 128 * h + 128]
+            points[w, first + 6 : first + 8, :] = jnp.ones((2, 128), jnp.float32)
+    raw_copy.wait()
+    for f in range(2):
+        img[f] = jnp.swapaxes(raw[f], 0, 1)
     pl.semaphore_wait(barrier, len(peers))
 
     sends = []
@@ -115,6 +119,53 @@
     for d, f in halo_peers:
         send(img.at[f], block(2 - 2 * d + t), h_sem.at[2 - 2 * d + t], at(p, (2 * (k + d) + f + 64) % 64))
 
+    def post(src, sem, number, device):
+        pltpu.make_async_remote_copy(
+            src_ref=src, dst_ref=src, send_sem=ag_send.at[number], recv_sem=sem,
+            device_id=device, device_id_type=MESH,
+        ).start()
+
+    class Spread:
+        def __init__(self, ref, z_sem, x_sem, f_sem, number):
+            self.ref, self.z_sem, self.x_sem, self.f_sem, self.number = ref, z_sem, x_sem, f_sem, number
+
+        def block(self, d, column=0):
+            return self.ref.at[16 * ((x + column + 4) % 4) + (z - d + 16) % 16]
+
+        def z_first(self):
+            for d in NEAR:
+                post(self.block(0), self.z_sem.at[d % 16], self.number, z_dev(d))
+
+        def z_wait(self, d):
+            arrived(self.block(d), self.z_sem.at[d % 16])
+
+        def z_second(self):
+            for d in (4, -4):
+                self.z_wait(d)
+                for e in (4, 3, 2, 1) if d > 0 else (-3, -2, -1):
+                    post(self.block(d), self.z_sem.at[(d + e) % 16], self.number, z_dev(e))
+
+        def x_first(self, d):
+            for side in range(2):
+                post(self.block(d), self.x_sem.at[side, d % 16], self.number, x_dev(1 - 2 * side))
+
+        def x_second(self, d):
+            for side in range(2):
+                step = 1 - 2 * side
+                arrived(self.block(d, -step), self.x_sem.at[side, d % 16])
+                if d % 2 == side:
+                    post(self.block(d, -step), self.f_sem, self.number, x_dev(step))
+
+        def end(self):
+            arrived(self.ref.at[pl.ds(16 * ((x + 2) % 4), 16)], self.f_sem)
+            pltpu.make_async_remote_copy(
+                src_ref=self.ref.at[pl.ds(0, 63)], dst_ref=self.ref.at[pl.ds(0, 63)],
+                send_sem=ag_send.at[self.number], recv_sem=own_sem, device_id=partner, device_id_type=MESH,
+            ).wait_send()
+
+    spread_points = Spread(points, pz_sem, px_sem, pf_sem, 0)
+    spread_table = Spread(table, tz_sem, tx_sem, tf_sem, 1)
+
     def q_cols(layer, owner, first=0, tiles=3):
         return weights.at[layer, :, pl.ds(pl.multiple_of(768 + 384 * owner + 128 * first, 128), 128 * tiles)]
 
@@ -133,6 +184,7 @@
         step = sign * (1 - 2 * d)
         send(a_cols(p), a_cols(p), y1_sem.at[d, 1], y_dev(step))
     send(weights.at[p], weights.at[p], d_sem.at[3], partner)
+    spread_points.z_first()
 
     q_parts = ((0, 2), (2, 1))
     a_parts = ((0, 3), (3, 3))
@@ -176,45 +228,11 @@
         x_done(near[d], d)
         send(weights.at[near[d]], weights.at[near[d]], d_sem.at[d], partner)
     x_second(far, 2)
+    spread_points.z_second()
     for d in range(2):
         arrived(a_cols(far, *a_parts[d]), y2_sem.at[d, 1])
     x_done(far, 2)
     send(weights.at[far], weights.at[far], d_sem.at[2], partner)
-
-    order = (8, 7, 9, 6, 10, 5, 11, 4, 12, 3, 13, 2, 14, 1, 15)
-
-    def spread_z(ref, sem, number):
-        own = ref.at[w]
-        for d in order:
-            pltpu.make_async_remote_copy(
-                src_ref=own, dst_ref=own, send_sem=ag_send.at[number], recv_sem=sem.at[d],
-                device_id=z_dev(d), device_id_type=MESH,
-            ).start()
-
-    def forward(ref, sem, source, number):
-        for e in (1, 2, 3):
-            pltpu.make_async_remote_copy(
-                src_ref=ref.at[source], dst_ref=ref.at[source], send_sem=ag_send.at[number], recv_sem=sem.at[e],
-                device_id=x_dev(e), device_id_type=MESH,
-            ).start()
-
-    def spread_x(ref, z_sem, x_sem, number):
-        forward(ref, x_sem, w, number)
-        for d in reversed(order):
-            source = 16 * x + (z - d + 16) % 16
-            arrived(ref.at[source], z_sem.at[d])
-            forward(ref, x_sem, source, number)
-
-    def spread_end(ref, x_sem, number):
-        for e in (1, 2, 3):
-            arrived(ref.at[pl.ds(16 * ((x - e + 4) % 4), 16)], x_sem.at[e])
-        pltpu.make_async_remote_copy(
-            src_ref=ref.at[pl.ds(0, 63)], dst_ref=ref.at[pl.ds(0, 63)], send_sem=ag_send.at[number],
-            recv_sem=own_sem, device_id=partner, device_id_type=MESH,
-        ).wait_send()
-
-    points[w] = pts[...]
-    spread_z(points, pz_sem, 0)
 
     act[0, pl.ds(pl.multiple_of((2 + t) * 256, 256), 256), :] = img[t]
     for j in (0, 1, 4, 5):
@@ -236,24 +254,51 @@
     for j in (3, 0, 1, 2):
         arrived(weights.at[theirs[j]], d_sem.at[j])
 
-    layers(act, weights, 0, 4, top_row)
-    spread_x(points, pz_sem, px_sem, 0)
-    layers(act, weights, 4, 8, top_row)
-
+    layers(act, weights, (0, 1), top_row)
+    for d in EARLY + LATE:
+        if d not in (0, 4, -4):
+            spread_points.z_wait(d)
+        spread_points.x_first(d)
+    layers(act, weights, (2, 3, 4, 5), top_row)
+    for d in EARLY + LATE:
+        spread_points.x_second(d)
+    layers(act, weights, (6, 7), top_row)
+
+    row_i = lax.broadcasted_iota(jnp.int32, (48, 11), 0)
+    row_j = lax.broadcasted_iota(jnp.int32, (48, 11), 1)
+    placed = []
+    for q in range(4):
+        here = jnp.where(row_i == row_j + 11 * q, 1.0, 0.0).astype(jnp.bfloat16)
+        placed.append(
+            jnp.dot(here, class_weight[...], preferred_element_type=jnp.float32).astype(jnp.bfloat16)
+        )
     total = None
     for q in range(4):
         part = lax.dot_general(
-            cwq[q], act[0, pl.ds(512 + 128 * q, 128), :], (((1,), (1,)), ((), ())),
+            placed[q], act[0, pl.ds(512 + 128 * q, 128), :], (((1,), (1,)), ((), ())),
             preferred_element_type=jnp.float32,
         )
         total = part if total is None else total + part
     table[w] = total.astype(jnp.bfloat16)
     sc[t] = total
-    spread_z(table, tz_sem, 1)
+    spread_table.z_first()
+    spread_table.x_first(0)
     send(sc.at[t], sc.at[t], s_sem, sibling)
-    spread_x(table, tz_sem, tx_sem, 1)
-    spread_end(points, px_sem, 0)
-    spread_end(table, tx_sem, 1)
+    spread_table.z_second()
+    spread_table.x_first(4)
+    spread_table.x_first(-4)
+    for d in (1, -1, 2, -2, 3, -3):
+        spread_table.z_wait(d)
+        spread_table.x_first(d)
+    for d in EARLY:
+        spread_table.x_second(d)
+    for d in LATE:
+        spread_table.z_wait(d)
+        spread_table.x_first(d)
+    for d in LATE:
+        spread_table.x_second(d)
+    spread_points.end()
+    spread_table.end()
     arrived(sc.at[1 - t], s_sem)
     for copy in sends:
         copy.wait_send()
@@ -262,8 +307,9 @@
 N_SENDS = 48
 
 
-def image_part(img, conv_weight, cwq, pts):
+def image_part(image, conv_weight, class_weight, feats, pixel, pillar, counts):
     vmem = pl.BlockSpec(memory_space=pltpu.VMEM)
+    hbm = pl.BlockSpec(memory_space=pltpu.HBM)
     dma = pltpu.SemaphoreType.DMA
     return pl.pallas_call(
         image_kernel,
@@ -273,19 +319,21 @@
             jax.ShapeDtypeStruct((64, 48, 128), jnp.bfloat16),
             jax.ShapeDtypeStruct((64, 32, 128), jnp.float32),
         ),
-        in_specs=[vmem, pl.BlockSpec(memory_space=pl.ANY), vmem, vmem],
+        in_specs=[hbm, hbm] + [vmem] * 5,
         out_specs=(vmem, vmem, vmem),
         scratch_shapes=[
             pltpu.VMEM((8, C, 9 * C), jnp.bfloat16),
-            pltpu.VMEM((2, BUF, C), jnp.bfloat16),
-            dma, dma((N_SENDS,)), dma((6,)), dma((2, 2)), dma((2, 2)), dma((2, 3)), dma((2, 3)), dma((4,)),
-            dma((16,)), dma((4,)), dma((16,)), dma((4,)), dma, dma((2,)),
+            pltpu.VMEM((2, ROWS * 64, C), jnp.bfloat16),
+            pltpu.VMEM((2, C, 256), jnp.bfloat16),
+            pltpu.VMEM((2, 256, C), jnp.bfloat16),
+            dma, dma, dma((N_SENDS,)), dma((6,)), dma((2, 2)), dma((2, 2)), dma((2, 3)), dma((2, 3)), dma((4,)),
+            dma((16,)), dma((2, 16)), dma, dma((16,)), dma((2, 16)), dma, dma, dma((2,)),
         ],
         compiler_params=pltpu.CompilerParams(
             collective_id=0, has_side_effects=True, vmem_limit_bytes=40 * 2**20
         ),
         cost_estimate=pl.CostEstimate(flops=10**10, bytes_accessed=10**7, transcendentals=0),
-    )(img, conv_weight, cwq, pts)
+    )(image, conv_weight, class_weight, feats, pixel, pillar, counts)
 
 
 SLOTS = 128
@@ -446,16 +494,10 @@
     bev_weight,
     head_weight,
 ):
-    p = lax.axis_index("phase")
     t = lax.axis_index("wide") % 2
-    img = jnp.swapaxes(lax.dynamic_slice_in_dim(image, 2 * p, 2, 0), 1, 2)
-    live = jnp.arange(256, dtype=jnp.int32)[None, :] < point_counts
-    cell = jnp.where(live, pillar_index, -1024)
-    used = jnp.ones((2, 1, 256), jnp.float32)
-    rows = [point_feats, pixel_index[:, None].astype(jnp.float32), cell[:, None].astype(jnp.float32), used, used]
-    pts = jnp.concatenate(rows, axis=1).reshape(2, 8, 2, 128).transpose(0, 2, 1, 3).reshape(32, 128)
-    cwq = jnp.stack([jnp.pad(class_weight, ((11 * q, 37 - 11 * q), (0, 0))) for q in range(4)])
-    sc, table, points = image_part(img, conv_weight, cwq, pts)
+    sc, table, points = image_part(
+        image, conv_weight, class_weight, point_feats, pixel_index, pillar_index, point_counts
+    )
     own = lax.dynamic_slice_in_dim(sc[:, :44].reshape(2, 4, 11, 128), 2 * t, 2, 1)
     scores = own.transpose(0, 2, 1, 3).reshape(2, 11, 256)
     raw, gates = pillar_weight[:, :4], jnp.pad(pillar_weight[:, 4:], ((0, 0), (0, 5)))

time: 115 us -> 103 us (0.90)
  the two profiles are of different devices: /device:TPU:1 before, /device:TPU:8 now
where the time goes in v2:
time: 103 us
  Pallas kernels  94.3 us (92%)
  local copies, waits for them, and re-layouts  8.05 us (8%)
    pallas_call x1, Pallas kernels, image_part(): pl.pallas_call(image_kernel, name='image_part', out_shape=(jax.ShapeDtype...  81 us
    pallas_call x1, Pallas kernels, point_part(): pl.pallas_call(point_kernel, name='point_part', out_shape=jax.ShapeDtypeS...  13.3 us
    unnamed x24, local copies, waits for them, and re-layouts  7.3 us

profile of v2, /device:TPU:8, one launch (start us, length us, event | category | flops | bytes accessed | tf_op | source)
XLA Modules:
  0.0 103.2 jit_solution(7386769967486148870)
XLA Ops:
  0.6 0.7 copy.24.counts
  1.4 0.0 copy-start
  1.4 1.6 %copy-done = bf16[16,256,256]{2,1,0:T(8,128)(2,1)S(1)} copy-done((bf16[16,256,256]{2,1,0:T(8,128)(2,1)S(1)}, bf16[16,256,256]{2,1,0:T(8,128)(2,1)}, u32[]{:S(2)}) %copy-start) | copy-done | bytes 2097176
  3.0 0.0 copy-start.1
  3.0 1.3 %copy-done.1 = bf16[1,256,2304]{2,1,0:T(8,128)(2,1)S(1)} copy-done((bf16[1,256,2304]{2,1,0:T(8,128)(2,1)S(1)}, bf16[1,256,2304]{2,1,0:T(8,128)(2,1)}, u32[]{:S(2)}) %copy-start.1) | copy-done | bytes 1179672
  4.2 0.0 copy-start.3
  4.3 0.7 copy-done.3
  4.9 0.7 copy-done.4
  5.6 0.7 copy-done.5
  6.3 0.7 copy-done.6
  7.0 0.0 copy-start.2
  7.0 81.0 %image_part.1 = (f32[2,48,128]{2,1,0:T(8,128)S(1)}, bf16[64,48,128]{2,1,0:T(8,128)(2,1)S(1)}, f32[64,32,128]{2,1,0:T(8,128)S(1)}) custom-call(bf16[16,256,256]{2,1,0:T(8,128)(2,1)S(1)} %copy-done, bf16[1,256,2304]{2,1,0:T(8,128)(2,1)S(1)} %copy-done.1, bf16[11,256]{1,0:T(8,128)(2,1)S(1)} %copy-done.3, f32[2,4,256]{2,1,0:T(4,128)S(1)} %copy-done.4, ...), custom_call_target="tpu_custom_call" | custom-call | flops 10000000000 | bytes 10000000 | tf_op jit(solution)/shard_map/image_part/pallas_call | solution.py:314
  88.1 0.6 copy_bitcast_fusion
  88.7 0.0 copy-done.8
  88.7 0.1 copy.31
  88.8 0.0 slice-done
  88.8 0.1 copy.25
  88.9 0.0 copy-done.9
  88.9 0.1 pad_maximum_fusion.wk
  89.0 0.0 copy-done.7
  89.0 0.1 copy.27.head
  89.2 0.0 copy-done.2
  89.2 13.3 %point_part.1 = f32[2,128,20]{2,1,0:T(8,128)S(1)} custom-call(f32[2048,128]{1,0:T(8,128)S(1)} %bitcast.10, bf16[64,48,128]{2,1,0:T(8,128)(2,1)S(1)} %get-tuple-element.6.table, f32[64,48]{1,0:T(8,128)S(1)} %pad_maximum_fusion.wk, bf16[576,384]{1,0:T(8,128)(2,1)S(1)} %copy-done.2, bf16[384,20]{1,0:T(8,128)(2,1)S(1)} %copy.27.head), custom_call_target="tpu_custom_call" | custom-call | flops 1000000000 | bytes 3000000 | tf_op jit(solution)/shard_map/point_part/pallas_call | solution.py:469
  102.5 0.7 copy.30
  (11 shorter events, 0.1 us)
Async XLA Ops:
  1.4 1.6 %copy-start = (bf16[16,256,256]{2,1,0:T(8,128)(2,1)S(1)}, bf16[16,256,256]{2,1,0:T(8,128)(2,1)}, u32[]{:S(2)}) copy-start(bf16[16,256,256]{2,1,0:T(8,128)(2,1)} %image.1) | copy-start | bytes 6291460
  3.0 1.3 %copy-start.1 = (bf16[1,256,2304]{2,1,0:T(8,128)(2,1)S(1)}, bf16[1,256,2304]{2,1,0:T(8,128)(2,1)}, u32[]{:S(2)}) copy-start(bf16[1,256,2304]{2,1,0:T(8,128)(2,1)} %w_own.1) | copy-start | bytes 3538948
  4.2 0.7 copy-start.3
  4.9 0.7 copy-start.4
  5.6 0.7 copy-start.5
  6.3 0.7 copy-start.6
  7.0 81.7 %copy-start.8 = (f32[64,15]{0,1:T(8,128)S(1)}, f32[64,15]{0,1:T(8,128)}, u32[]{:S(2)}) copy-start(f32[64,15]{0,1:T(8,128)} %param.17) | copy-start | bytes 11524
  7.0 81.8 %slice-start = ((f32[64,15]{0,1:T(8,128)}), f32[64,8]{0,1:T(8,128)S(1)}, s32[]{:S(2)}) async-start(f32[64,15]{0,1:T(8,128)} %param.17), calls=%async_computation | async-start | bytes 8192 | tf_op jit(solution)/shard_map/slice
  7.0 81.9 %copy-start.9 = (pred[8]{0:T(512)(128)(4,1)S(1)}, pred[8]{0:T(512)(128)(4,1)}, u32[]{:S(2)}) copy-start(pred[8]{0:T(512)(128)(4,1)} %constant.17.clone.1) | copy-start | bytes 28
  7.0 82.0 %copy-start.7 = (bf16[384,20]{0,1:T(8,128)(2,1)S(1)}, bf16[384,20]{0,1:T(8,128)(2,1)}, u32[]{:S(2)}) copy-start(bf16[384,20]{0,1:T(8,128)(2,1)} %param.19) | copy-start | bytes 46084
  7.0 82.1 %copy-start.2 = (bf16[576,384]{1,0:T(8,128)(2,1)S(1)}, bf16[576,384]{1,0:T(8,128)(2,1)}, u32[]{:S(2)}) copy-start(bf16[576,384]{1,0:T(8,128)(2,1)} %bev.1) | copy-start | bytes 1327108

commit v3 on v2

v3 whole, which is shorter than its diff:
```python
import functools

import jax
import jax.numpy as jnp
from jax import lax
from jax.experimental import pallas as pl
from jax.experimental.pallas import tpu as pltpu
from jax.sharding import PartitionSpec as P

C = 256
ROWS = 24
MOST_ROWS = 12
MESH = pl.DeviceIdType.MESH
NEAR = (4, -4, 3, -3, 2, -2, 1, -1)
EARLY = (0, 4, -4, 1, -1, 2, -2, 3, -3)
LATE = (5, -5, 6, -6, 7, -7, 8)


SLOTS = 128
GROUP = 16
LANES = 256


def iota(shape, dim):
    return lax.broadcasted_iota(jnp.int32, shape, dim).astype(jnp.float32)


def where_bf16(mask):
    return jnp.where(mask, jnp.float32(1.0), jnp.float32(0.0)).astype(jnp.bfloat16)


def split(value):
    high = value.astype(jnp.bfloat16)
    return high, (value - high.astype(jnp.float32)).astype(jnp.bfloat16)


def find_places(points, place, f, first_cell):
    row_i = lax.broadcasted_iota(jnp.int32, (128, 128), 0)
    col_i = lax.broadcasted_iota(jnp.int32, (128, 128), 1)
    up_to = where_bf16(row_i <= col_i)
    row_j = lax.broadcasted_iota(jnp.int32, (64, 64), 0)
    col_j = lax.broadcasted_iota(jnp.int32, (64, 64), 1)
    before = where_bf16((row_j // GROUP == col_j // GROUP) & (col_j < row_j))
    all_ones = jnp.ones((128, 128), jnp.bfloat16)
    for h in range(2):
        cell = points[pl.ds((2 * f + h) * 8 + 5, 64, stride=32), :] - first_cell
        mine = (cell >= 0.0) & (cell < 384.0)
        mine_16 = where_bf16(mine)
        inside = jnp.dot(mine_16, up_to, preferred_element_type=jnp.float32)
        row_sum = jnp.dot(mine_16, all_ones, preferred_element_type=jnp.float32)
        ahead = jnp.dot(before, row_sum.astype(jnp.bfloat16), preferred_element_type=jnp.float32)
        place[2 * f + h] = jnp.where(mine, inside - 1.0 + ahead, -1.0)


def pack_group(points, place, packed, f, g, first_slot, where):
    h, first = g // 4, pl.multiple_of(g % 4 * GROUP, GROUP)
    slot = iota((SLOTS, 128), 0) + first_slot
    places = place[2 * f + h, pl.ds(first, GROUP), :]
    data, picks = [], []
    for i in range(GROUP):
        rows = points[pl.ds(pl.multiple_of((first + i) * 32 + (2 * f + h) * 8, 8), 8), :]
        high, low = split(rows)
        data.append(jnp.concatenate([high.astype(jnp.float32), low.astype(jnp.float32)], axis=0))
        picks.append(where_bf16(slot == places[i : i + 1, :]))
    packed[where] = lax.dot_general(
        jnp.concatenate(data, axis=1).astype(jnp.bfloat16), jnp.concatenate(picks, axis=1),
        (((1,), (1,)), ((), ())), preferred_element_type=jnp.float32,
    )


def layers(act, weights, numbers, top_row):
    for number in numbers:
        now, later = number % 2, (number + 1) % 2
        rows = 22 - 2 * number
        half = rows if rows <= MOST_ROWS else (rows + 1) // 2
        for first in range(0, rows, half):
            count = min(half, rows - first) * 64
            start = (number + 1 + first) * 64
            column = lax.broadcasted_iota(jnp.int32, (count, 1), 0) % 64
            row = lax.broadcasted_iota(jnp.int32, (count, 1), 0) // 64 + (top_row + number + 1 + first)
            lhs = jnp.concatenate([act[now, pl.ds(start + 64 * r, count), :] for r in (-1, 0, 1)], axis=1)

            def part(tap):
                rhs = jnp.concatenate(
                    [weights[number, :, (3 * r + tap) * C : (3 * r + tap + 1) * C] for r in range(3)], axis=1
                )
                return lax.dot_general(lhs, rhs, (((1,), (1,)), ((), ())), preferred_element_type=jnp.float32)

            total = part(1)
            total = total + jnp.where(column >= 1, pltpu.roll(part(0), 1, 0), 0.0)
            total = total + jnp.where(column < 63, pltpu.roll(part(2), count - 1, 0), 0.0)
            new = act[now, pl.ds(start, count), :].astype(jnp.float32) + jnp.maximum(total, 0.0)
            new = jnp.where((row >= 0) & (row < 256), new, 0.0)
            act[later, pl.ds(start, count), :] = new.astype(jnp.bfloat16)


def image_kernel(
    image, w_own, class_weight_h, feats_h, pixel_h, pillar_h, counts_h, sc, table, points, packed, place, weights, act, raw, img,
    class_weight, feats, pixel, pillar, counts, own_sem, raw_sem, in_sem, send_sem, h_sem, y1_sem, y2_sem, x1_sem, x2_sem, d_sem, tz_sem, tx_sem, tf_sem,
    pz_sem, px_sem, pf_sem, s_sem, ag_send,
):
    p = lax.axis_index("phase")
    w = lax.axis_index("wide")
    y, c = p // 2, p % 2
    x, z = w // 16, w % 16
    k, t = w // 2, w % 2
    top_row = 8 * k - 8

    def at(phase, wide):
        return {"phase": phase, "wide": wide}

    def y_dev(step):
        return at(2 * ((y + step + 4) % 4) + c, w)

    def x_dev(step):
        return at(p, 16 * ((x + step + 4) % 4) + z)

    def z_dev(step):
        return at(p, 16 * x + (z + step + 16) % 16)

    partner = at(2 * y + 1 - c, w)
    sibling = at(p, 2 * k + 1 - t)
    halo_peers = [(d, f) for d in (-1, 1) for f in (0, 1)]

    raw_copy = pltpu.make_async_copy(image.at[pl.ds(2 * p, 2)], raw, raw_sem)
    raw_copy.start()
    own_copy = pltpu.make_async_copy(w_own.at[0], weights.at[p], own_sem)
    own_copy.start()
    small = [
        pltpu.make_async_copy(src, dst, in_sem.at[i])
        for i, (src, dst) in enumerate(
            ((feats_h, feats), (pixel_h, pixel), (pillar_h, pillar), (counts_h, counts), (class_weight_h, class_weight))
        )
    ]
    for copy in small:
        copy.start()
    barrier = pltpu.get_barrier_semaphore()
    peers = [y_dev(1), y_dev(-1), partner, sibling]
    peers += [x_dev(1), x_dev(-1)] + [z_dev(d) for d in NEAR]
    peers += [at(p, (2 * (k + d) + f + 64) % 64) for d, f in halo_peers]
    for peer in peers:
        pl.semaphore_signal(barrier, inc=1, device_id=peer, device_id_type=MESH)
    for copy in small:
        copy.wait()
    lane = lax.broadcasted_iota(jnp.int32, (1, 256), 1)
    for f in range(2):
        cell = jnp.where(lane < counts[:, f : f + 1], pillar[f : f + 1, :], -1024).astype(jnp.float32)
        where = pixel[f : f + 1, :].astype(jnp.float32)
        for h in range(2):
            first = 32 * w + (2 * f + h) * 8
            points[pl.ds(first, 4), :] = feats[f, :, 128 * h : 128 * h + 128]
            points[pl.ds(first + 4, 1), :] = where[:, 128 * h : 128 * h + 128]
            points[pl.ds(first + 5, 1), :] = cell[:, 128 * h : 128 * h + 128]
            points[pl.ds(first + 6, 2), :] = jnp.ones((2, 128), jnp.float32)
    raw_copy.wait()
    for f in range(2):
        img[f] = jnp.swapaxes(raw[f], 0, 1)
    pl.semaphore_wait(barrier, len(peers))

    sends = []

    def send(src, dst, recv, device):
        number = len(sends)
        copy = pltpu.make_async_remote_copy(
            src_ref=src, dst_ref=dst, send_sem=send_sem.at[number], recv_sem=recv,
            device_id=device, device_id_type=MESH,
        )
        copy.start()
        sends.append(copy)

    def arrived(ref, recv):
        pltpu.make_async_remote_copy(
            src_ref=ref, dst_ref=ref, send_sem=send_sem.at[0], recv_sem=recv,
            device_id=partner, device_id_type=MESH,
        ).wait_recv()

    def block(j):
        return act.at[0, pl.ds(pl.multiple_of(j * 256, 256), 256), :]

    send(img.at[1 - t], block(2 + t), h_sem.at[2 + t], sibling)
    for d, f in halo_peers:
        send(img.at[f], block(2 - 2 * d + t), h_sem.at[2 - 2 * d + t], at(p, (2 * (k + d) + f + 64) % 64))

    def post(src, sem, number, device):
        pltpu.make_async_remote_copy(
            src_ref=src, dst_ref=src, send_sem=ag_send.at[number], recv_sem=sem,
            device_id=device, device_id_type=MESH,
        ).start()

    class Spread:
        def __init__(self, ref, rows, z_sem, x_sem, f_sem, number):
            self.ref, self.rows, self.number = ref, rows, number
            self.z_sem, self.x_sem, self.f_sem = z_sem, x_sem, f_sem

        def block(self, d, column=0):
            return self.some(16 * ((x + column + 4) % 4) + (z - d + 16) % 16, 1)

        def some(self, first, count):
            return self.ref.at[pl.ds(pl.multiple_of(self.rows * first, self.rows), self.rows * count)]

        def z_first(self):
            for d in NEAR:
                post(self.block(0), self.z_sem.at[d % 16], self.number, z_dev(d))

        def z_wait(self, d):
            arrived(self.block(d), self.z_sem.at[d % 16])

        def z_second(self):
            for d in (4, -4):
                self.z_wait(d)
                for e in (4, 3, 2, 1) if d > 0 else (-3, -2, -1):
                    post(self.block(d), self.z_sem.at[(d + e) % 16], self.number, z_dev(e))

        def x_first(self, d):
            for side in range(2):
                post(self.block(d), self.x_sem.at[side, d % 16], self.number, x_dev(1 - 2 * side))

        def x_second(self, d):
            for side in range(2):
                step = 1 - 2 * side
                arrived(self.block(d, -step), self.x_sem.at[side, d % 16])
                if d % 2 == side:
                    post(self.block(d, -step), self.f_sem, self.number, x_dev(step))

        def last(self):
            arrived(self.some(16 * ((x + 2) % 4), 16), self.f_sem)

        def sent(self):
            pltpu.make_async_remote_copy(
                src_ref=self.some(0, 63), dst_ref=self.some(0, 63),
                send_sem=ag_send.at[self.number], recv_sem=own_sem, device_id=partner, device_id_type=MESH,
            ).wait_send()

    spread_points = Spread(points, 32, pz_sem, px_sem, pf_sem, 0)
    spread_table = Spread(table, 48, tz_sem, tx_sem, tf_sem, 1)

    def q_cols(layer, owner, first=0, tiles=3):
        return weights.at[layer, :, pl.ds(pl.multiple_of(768 + 384 * owner + 128 * first, 128), 128 * tiles)]

    def a_cols(layer, half):
        return weights.at[layer, :, pl.ds(384 * half, 384)]

    def layer_of(step):
        return 2 * ((y + step + 8) % 4) + c

    q_parts = ((0, 2), (2, 1))
    sign = 1 - 2 * c
    steps = (sign, -sign)
    near = [layer_of(-sign), layer_of(sign)]
    far = layer_of(2)
    soon_step = 1 - 2 * (((y + 1) // 2) % 2)
    soon = (1 + soon_step * sign) // 2
    late = 1 - soon
    soon_layer, late_layer = layer_of(soon_step), layer_of(-soon_step)

    def x_first(layer, j):
        for d in range(2):
            send(q_cols(layer, x), q_cols(layer, x), x1_sem.at[d, j], x_dev(steps[d]))

    def x_second(layer, j):
        for d in range(2):
            source = (x - steps[d] + 4) % 4
            arrived(q_cols(layer, source), x1_sem.at[d, j])
            part = q_cols(layer, source, *q_parts[d])
            send(part, part, x2_sem.at[d, j], x_dev(steps[d]))

    def x_done(layer, j):
        for d in range(2):
            arrived(q_cols(layer, (x + 2) % 4, *q_parts[d]), x2_sem.at[d, j])

    def hand_over(layer, half):
        part = weights.at[layer, :, pl.ds(768 * half, 768 + 768 * half)]
        send(part, part, d_sem.at[layer // 2, half], partner)

    def taken_over(number):
        @pl.when(c == 1 - number % 2)
        def _():
            for half in range(2):
                arrived(weights.at[number, :, pl.ds(768 * half, 768 + 768 * half)], d_sem.at[number // 2, half])

    own_copy.wait()
    for d in range(2):
        send(q_cols(p, x), q_cols(p, x), y1_sem.at[d, 0], y_dev(steps[d]))
    for d in range(2):
        send(a_cols(p, d), a_cols(p, d), y1_sem.at[d, 1], y_dev(steps[d]))
    hand_over(p, 0)
    hand_over(p, 1)
    spread_points.z_first()
    for d in range(2):
        arrived(q_cols(near[d], x), y1_sem.at[d, 0])
        part = q_cols(near[d], x, *q_parts[d])
        send(part, part, y2_sem.at[d, 0], y_dev(steps[d]))
    x_first(soon_layer, soon)
    for d in range(2):
        arrived(a_cols(near[d], d), y1_sem.at[d, 1])
        send(a_cols(near[d], d), a_cols(near[d], d), y2_sem.at[d, 1], y_dev(steps[d]))
        send(a_cols(p, 1 - d), a_cols(p, 1 - d), y1_sem.at[d, 2], y_dev(steps[d]))
    for d in range(2):
        arrived(q_cols(far, x, *q_parts[d]), y2_sem.at[d, 0])
    x_first(far, 2)
    x_second(soon_layer, soon)
    x_second(far, 2)
    x_first(late_layer, late)
    for d in range(2):
        arrived(a_cols(far, d), y2_sem.at[d, 1])
    hand_over(far, 0)
    spread_points.z_second()
    for d in range(2):
        arrived(a_cols(near[d], 1 - d), y1_sem.at[d, 2])
    hand_over(soon_layer, 0)
    hand_over(late_layer, 0)
    x_done(soon_layer, soon)
    hand_over(soon_layer, 1)
    x_done(far, 2)
    hand_over(far, 1)

    act[0, pl.ds(pl.multiple_of((2 + t) * 256, 256), 256), :] = img[t]
    for j in (0, 1, 4, 5):
        arrived(block(j), h_sem.at[j])
    arrived(block(3 - t), h_sem.at[3 - t])

    @pl.when(k == 0)
    def _():
        act[0, pl.ds(0, 512), :] = jnp.zeros((512, C), jnp.bfloat16)

    @pl.when(k == 31)
    def _():
        act[0, pl.ds(1024, 512), :] = jnp.zeros((512, C), jnp.bfloat16)

    def layer(number):
        taken_over(number)
        layers(act, weights, (number,), top_row)

    layer(0)
    layer(1)
    x_second(late_layer, late)
    for d in EARLY + LATE:
        if d not in (0, 4, -4):
            spread_points.z_wait(d)
        spread_points.x_first(d)
    layer(2)
    x_done(late_layer, late)
    hand_over(late_layer, 1)
    layer(3)
    layer(4)
    for d in EARLY + LATE:
        spread_points.x_second(d)
    layer(5)
    layer(6)
    layer(7)

    row_i = lax.broadcasted_iota(jnp.int32, (48, 11), 0)
    row_j = lax.broadcasted_iota(jnp.int32, (48, 11), 1)
    placed = []
    for q in range(4):
        here = jnp.where(row_i == row_j + 11 * q, 1.0, 0.0).astype(jnp.bfloat16)
        placed.append(
            jnp.dot(here, class_weight[...], preferred_element_type=jnp.float32).astype(jnp.bfloat16)
        )
    total = None
    for q in range(4):
        part = lax.dot_general(
            placed[q], act[0, pl.ds(512 + 128 * q, 128), :], (((1,), (1,)), ((), ())),
            preferred_element_type=jnp.float32,
        )
        total = part if total is None else total + part
    table[pl.ds(pl.multiple_of(48 * w, 48), 48), :] = total.astype(jnp.bfloat16)
    sc[t] = total
    spread_table.z_first()
    spread_table.x_first(0)
    send(sc.at[t], sc.at[t], s_sem, sibling)
    spread_points.last()
    first_cell = ((w - 1) * 128).astype(jnp.float32)
    for f in range(2):
        find_places(points, place, f, first_cell)

    def pack(first, last):
        def one(g, state):
            pack_group(points, place, packed, g // 8, g % 8, 0.0, g)
            return state

        lax.fori_loop(first, last, one, 0)

    pack(0, 4)
    spread_table.z_second()
    spread_table.x_first(4)
    spread_table.x_first(-4)
    for d in (1, -1, 2, -2, 3, -3):
        spread_table.z_wait(d)
        spread_table.x_first(d)
    pack(4, 8)
    for d in EARLY:
        spread_table.x_second(d)
    for d in LATE:
        spread_table.z_wait(d)
        spread_table.x_first(d)
    pack(8, 16)
    for d in LATE:
        spread_table.x_second(d)
    spread_points.sent()
    spread_table.last()
    spread_table.sent()
    arrived(sc.at[1 - t], s_sem)
    for copy in sends:
        copy.wait_send()


N_SENDS = 48


def image_part(image, conv_weight, class_weight, feats, pixel, pillar, counts):
    vmem = pl.BlockSpec(memory_space=pltpu.VMEM)
    hbm = pl.BlockSpec(memory_space=pltpu.HBM)
    dma = pltpu.SemaphoreType.DMA
    operands = (image, conv_weight, class_weight, feats, pixel, pillar, counts.reshape(1, 2))
    operands = [pltpu.with_memory_space_constraint(o, pltpu.HBM) for o in operands]
    return pl.pallas_call(
        image_kernel,
        name="image_part",
        out_shape=(
            jax.ShapeDtypeStruct((2, 48, 128), jnp.float32),
            jax.ShapeDtypeStruct((64 * 48, 128), jnp.bfloat16),
            jax.ShapeDtypeStruct((64 * 32, 128), jnp.float32),
            jax.ShapeDtypeStruct((16, 16, SLOTS), jnp.float32),
            jax.ShapeDtypeStruct((4, 64, 128), jnp.float32),
        ),
        in_specs=[hbm] * 7,
        out_specs=(vmem,) * 5,
        scratch_shapes=[
            pltpu.VMEM((8, C, 9 * C), jnp.bfloat16),
            pltpu.VMEM((2, ROWS * 64, C), jnp.bfloat16),
            pltpu.VMEM((2, C, 256), jnp.bfloat16),
            pltpu.VMEM((2, 256, C), jnp.bfloat16),
            pltpu.VMEM((11, C), jnp.bfloat16),
            pltpu.VMEM((2, 4, 256), jnp.float32),
            pltpu.VMEM((2, 256), jnp.int32),
            pltpu.VMEM((2, 256), jnp.int32),
            pltpu.VMEM((1, 2), jnp.int32),
            dma, dma, dma((5,)), dma((N_SENDS,)), dma((6,)), dma((2, 3)), dma((2, 2)), dma((2, 3)), dma((2, 3)), dma((4, 2)),
            dma((16,)), dma((2, 16)), dma, dma((16,)), dma((2, 16)), dma, dma, dma((2,)),
        ],
        compiler_params=pltpu.CompilerParams(
            collective_id=0, has_side_effects=True, vmem_limit_bytes=40 * 2**20
        ),
        cost_estimate=pl.CostEstimate(flops=10**10, bytes_accessed=10**7, transcendentals=0),
    )(*operands)


def point_kernel(points, table, packed_first, place, sc, wk, bev, head, out, scores, packed, pooled, found):
    w = lax.axis_index("wide")
    first_cell = ((w - 1) * 128).astype(jnp.float32)
    low_row = iota((128, LANES), 0)
    quarter_row = lax.broadcasted_iota(jnp.int32, (48, LANES), 0) // 11
    quarter_row = quarter_row.astype(jnp.float32)
    class_i = lax.broadcasted_iota(jnp.int32, (16, 48), 0)
    class_j = lax.broadcasted_iota(jnp.int32, (16, 48), 1)
    to_class = where_bf16((class_j % 11 == class_i) & (class_j < 44))
    wk_high, wk_low = split(wk[...])
    wk_both = jnp.concatenate([wk_high, wk_low], axis=0)
    column = lax.broadcasted_iota(jnp.int32, (128, 1), 0)

    def frame(f, carry):
        most = jnp.max(jnp.maximum(place[2 * f], place[2 * f + 1])) + 1.0
        passes = (most.astype(jnp.int32) + SLOTS - 1) // SLOTS
        packed[...] = packed_first[pl.ds(8 * f, 8)]
        pooled[...] = jnp.zeros_like(pooled)

        def one_pass(number, inner):
            @pl.when(number > 0)
            def _():
                def group(g, state):
                    pack_group(points, place, packed, f, g, (number * SLOTS).astype(jnp.float32), g)
                    return state

                lax.fori_loop(0, 8, group, 0)

            def lanes(s, state):
                chosen = jnp.concatenate([packed[2 * s], packed[2 * s + 1]], axis=1)
                value = chosen[:8] + chosen[8:]
                pixel, cell, used = value[4:5], value[5:6] - first_cell, value[6:7]
                block = jnp.floor(pixel * (1.0 / 128.0))
                low = pixel - 128.0 * block
                pair = jnp.floor(block * 0.25)
                quarter = block - 4.0 * pair
                of_frame = jnp.concatenate([table[pl.ds(pl.multiple_of((2 * i + f) * 48, 48), 48), :] for i in range(32)], axis=0)
                read = jnp.dot(of_frame, where_bf16(low_row == low), preferred_element_type=jnp.float32)
                total = jnp.zeros((48, LANES), jnp.float32)
                for i in range(32):
                    total = total + jnp.where(pair == float(i), read[48 * i : 48 * i + 48], 0.0)
                total = jnp.where(quarter_row == quarter, total, 0.0)
                painted = jnp.dot(to_class, total.astype(jnp.bfloat16), preferred_element_type=jnp.float32)
                gate = jax.nn.sigmoid(painted)
                gate_high, gate_low = split(gate)
                features = jnp.concatenate([chosen.astype(jnp.bfloat16), gate_high, gate_low], axis=0)
                both = jnp.dot(wk_both, features, preferred_element_type=jnp.float32)
                hidden = jnp.maximum(both[:64] + both[64:], 0.0)
                row = jnp.floor(cell * (1.0 / 128.0))
                col = cell - 128.0 * row
                row = jnp.where(used > 0.5, row, -1.0)
                by_row = jnp.concatenate(
                    [jnp.where(row == float(r), hidden, 0.0) for r in range(3)], axis=0
                ).astype(jnp.bfloat16)
                pooled[...] += lax.dot_general(
                    where_bf16(low_row == col), by_row, (((1,), (1,)), ((), ())),
                    preferred_element_type=jnp.float32,
                )
                return state

            lax.fori_loop(0, 8 * SLOTS // LANES, lanes, 0)
            return inner

        lax.fori_loop(0, passes, one_pass, 0)
        grid = pooled[...]
        total = None
        for d in range(3):
            if d == 0:
                moved = jnp.where(column >= 1, pltpu.roll(grid, 1, 0), 0.0)
            elif d == 2:
                moved = jnp.where(column < 127, pltpu.roll(grid, 127, 0), 0.0)
            else:
                moved = grid
            weight = jnp.concatenate([bev[(3 * r + d) * 64 : (3 * r + d + 1) * 64, :] for r in range(3)], axis=0)
            part = jnp.dot(moved.astype(jnp.bfloat16), weight, preferred_element_type=jnp.float32)
            total = part if total is None else total + part
        feature = jnp.maximum(total, 0.0).astype(jnp.bfloat16)
        found[f] = lax.dot_general(
            head[...], feature, (((1,), (1,)), ((), ())), preferred_element_type=jnp.float32
        )
        return carry

    lax.fori_loop(0, 2, frame, 0)
    for f in range(2):
        out[:, f, :] = found[f]
        for half in range(2):
            even, odd = sc[f, 11 * half : 11 * half + 11, :], sc[f, 11 * half + 22 : 11 * half + 33, :]
            scores[:, f, 128 * half : 128 * half + 128] = jnp.where(w % 2 == 0, even, odd)


def point_part(points, table, packed, place, sc, wk, bev, head):
    vmem = pl.BlockSpec(memory_space=pltpu.VMEM)
    return pl.pallas_call(
        point_kernel,
        name="point_part",
        out_shape=(
            jax.ShapeDtypeStruct((20, 2, 128), jnp.float32),
            jax.ShapeDtypeStruct((11, 2, 256), jnp.float32),
        ),
        in_specs=[vmem] * 8,
        out_specs=(vmem, vmem),
        scratch_shapes=[
            pltpu.VMEM((8, 16, SLOTS), jnp.float32),
            pltpu.VMEM((128, 192), jnp.float32),
            pltpu.VMEM((2, 20, 128), jnp.float32),
        ],
        compiler_params=pltpu.CompilerParams(vmem_limit_bytes=40 * 2**20),
        cost_estimate=pl.CostEstimate(flops=10**9, bytes_accessed=3 * 10**6, transcendentals=10**5),
    )(points, table, packed, place, sc, wk, bev, head)


def local(
    image,
    conv_weight,
    class_weight,
    point_feats,
    pixel_index,
    pillar_index,
    point_counts,
    pillar_weight,
    bev_weight,
    head_weight,
):
    sc, table, points, packed, place = image_part(
        image, conv_weight, class_weight, point_feats, pixel_index, pillar_index, point_counts
    )
    raw, gates = pillar_weight[:, :4], jnp.pad(pillar_weight[:, 4:], ((0, 0), (0, 5)))
    raw = jnp.pad(raw, ((0, 0), (0, 4)))
    wk = jnp.concatenate([raw, raw, gates, gates], axis=1)
    detections, scores = point_part(points, table, packed, place, sc, wk, bev_weight, head_weight.T)
    return (detections.transpose(1, 2, 0), scores.transpose(1, 0, 2))


def solution(mesh):
    placed = (
        P(None, None, "wide"),
        P("phase", None, None),
        P(),
        P("phase", None, "wide"),
        P("phase", "wide"),
        P("phase", "wide"),
        P("phase", "wide"),
        P(),
        P(),
        P(),
    )
    return jax.shard_map(
        local,
        mesh=mesh,
        in_specs=placed,
        out_specs=(P("phase", "wide", None), P("phase", None, "wide")),
        check_vma=False,
    )
```

time: 103 us -> 87.9 us (0.85)
  Pallas kernels: 94.3 us -> 84.7 us
  local copies, waits for them, and re-layouts: 8.05 us -> 1.59 us
    unnamed x24 -> x5, local copies, waits for them, and re-layouts: 7.3 us -> 0.11 us
    pallas_call x1, Pallas kernels: 81 us -> 75.6 us  [image_part(): pl.pallas_call(image_kernel, name='image_part', out_shape=(jax.ShapeDtype...]
    pallas_call x1, Pallas kernels: 13.3 us -> 9 us  [point_part(): pl.pallas_call(point_kernel, name='point_part', out_shape=(jax.ShapeDtype...]
where the time goes in v3:
time: 87.9 us; the launch traced here: 87.7 us
  Pallas kernels  84.7 us (96%)
  local copies, waits for them, and re-layouts  1.59 us (2%)
    pallas_call x1, Pallas kernels, image_part(): pl.pallas_call(image_kernel, name='image_part', out_shape=(jax.ShapeDtype...  75.6 us
    pallas_call x1, Pallas kernels, point_part(): pl.pallas_call(point_kernel, name='point_part', out_shape=(jax.ShapeDtype...  9 us

profile of v3, /device:TPU:8, one launch (start us, length us, event | category | flops | bytes accessed | tf_op | source)
XLA Modules:
  0.0 87.7 jit_solution(13456846498880546119)
XLA Ops:
  0.6 0.7 slice.7
  1.3 0.7 slice.8
  2.0 0.1 copy.14
  2.1 0.1 copy.12
  2.2 0.7 broadcast_select_fusion
  2.9 0.1 pad_maximum_fusion.wk
  3.0 0.0 copy-start
  3.0 0.0 copy-start.1
  3.0 75.6 %image_part.1 = (f32[2,48,128]{2,1,0:T(8,128)S(1)}, bf16[3072,128]{1,0:T(8,128)(2,1)S(1)}, f32[2048,128]{1,0:T(8,128)S(1)}, f32[16,16,128]{2,1,0:T(8,128)S(1)}, f32[4,64,128]{2,1,0:T(8,128)S(1)}) custom-call(bf16[16,256,256]{2,1,0:T(8,128)(2,1)} %image.1, bf16[1,256,2304]{2,1,0:T(8,128)(2,1)} %w_own.1, bf16[11,256]{1,0:T(8,128)(2,1)} %class_weight_h.1, ...), custom_call_target="tpu_custom_call" | custom-call | flops 10000000000 | bytes 10000000 | tf_op jit(solution)/shard_map/image_part/pallas_call | solution.py:417
  78.6 0.0 copy-done
  78.7 0.0 copy-done.1
  78.7 9.0 %point_part.1 = (f32[20,2,128]{2,1,0:T(2,128)}, f32[11,2,256]{2,1,0:T(2,128)}) custom-call(f32[2048,128]{1,0:T(8,128)S(1)} %get-tuple-element.9.points, bf16[3072,128]{1,0:T(8,128)(2,1)S(1)} %get-tuple-element.10.table, f32[16,16,128]{2,1,0:T(8,128)S(1)} %get-tuple-element.11.packed_first, f32[4,64,128]{2,1,0:T(8,128)S(1)} %get-tuple-element.12.place, ...), custom_call_target="tpu_custom_call" | custom-call | flops 1000000000 | bytes 3000000 | tf_op jit(solution)/shard_map/point_part/pallas_call | solution.py:541
  (1 shorter events, 0.0 us)
Async XLA Ops:
  3.0 75.7 %copy-start = (bf16[576,384]{1,0:T(8,128)(2,1)S(1)}, bf16[576,384]{1,0:T(8,128)(2,1)}, u32[]{:S(2)}) copy-start(bf16[576,384]{1,0:T(8,128)(2,1)} %bev.1) | copy-start | bytes 1327108
  3.0 75.7 %copy-start.1 = (bf16[384,20]{0,1:T(8,128)(2,1)S(1)}, bf16[384,20]{0,1:T(8,128)(2,1)}, u32[]{:S(2)}) copy-start(bf16[384,20]{0,1:T(8,128)(2,1)} %param.19) | copy-start | bytes 46084

commit v4 on v3

--- a/solution.py
+++ b/solution.py
@@ -18,7 +18,7 @@
 
 SLOTS = 128
 GROUP = 16
-LANES = 256
+LANES = 1024
 
 
 def iota(shape, dim):
@@ -281,8 +281,6 @@
     own_copy.wait()
     for d in range(2):
         send(q_cols(p, x), q_cols(p, x), y1_sem.at[d, 0], y_dev(steps[d]))
-    for d in range(2):
-        send(a_cols(p, d), a_cols(p, d), y1_sem.at[d, 1], y_dev(steps[d]))
     hand_over(p, 0)
     hand_over(p, 1)
     spread_points.z_first()
@@ -291,6 +289,8 @@
         part = q_cols(near[d], x, *q_parts[d])
         send(part, part, y2_sem.at[d, 0], y_dev(steps[d]))
     x_first(soon_layer, soon)
+    for d in range(2):
+        send(a_cols(p, d), a_cols(p, d), y1_sem.at[d, 1], y_dev(steps[d]))
     for d in range(2):
         arrived(a_cols(near[d], d), y1_sem.at[d, 1])
         send(a_cols(near[d], d), a_cols(near[d], d), y2_sem.at[d, 1], y_dev(steps[d]))
@@ -446,7 +446,7 @@
     )(*operands)
 
 
-def point_kernel(points, table, packed_first, place, sc, wk, bev, head, out, scores, packed, pooled, found):
+def point_kernel(points, table, packed_first, place, sc, pillar, bev, head, out, scores, packed, pooled, spare):
     w = lax.axis_index("wide")
     first_cell = ((w - 1) * 128).astype(jnp.float32)
     low_row = iota((128, LANES), 0)
@@ -455,62 +455,64 @@
     class_i = lax.broadcasted_iota(jnp.int32, (16, 48), 0)
     class_j = lax.broadcasted_iota(jnp.int32, (16, 48), 1)
     to_class = where_bf16((class_j % 11 == class_i) & (class_j < 44))
-    wk_high, wk_low = split(wk[...])
+    spare[...] = jnp.zeros_like(spare)
+    for first in (0, 8):
+        spare[first : first + 4, :64] = pillar[:4, :]
+    for first in (16, 32):
+        spare[first : first + 11, :64] = pillar[4:, :]
+    wk_high, wk_low = split(jnp.swapaxes(spare[...], 0, 1)[:64, :48])
     wk_both = jnp.concatenate([wk_high, wk_low], axis=0)
     column = lax.broadcasted_iota(jnp.int32, (128, 1), 0)
 
-    def frame(f, carry):
+    def contribution(f, source, first):
+        chosen = jnp.concatenate([source[first + i] for i in range(8)], axis=1)
+        value = chosen[:8] + chosen[8:]
+        pixel, cell, used = value[4:5], value[5:6] - first_cell, value[6:7]
+        block = jnp.floor(pixel * (1.0 / 128.0))
+        low = pixel - 128.0 * block
+        pair = jnp.floor(block * 0.25)
+        quarter = block - 4.0 * pair
+        of_frame = jnp.concatenate([table[pl.ds(pl.multiple_of((2 * i + f) * 48, 48), 48), :] for i in range(32)], axis=0)
+        read = jnp.dot(of_frame, where_bf16(low_row == low), preferred_element_type=jnp.float32)
+        total = jnp.zeros((48, LANES), jnp.float32)
+        for i in range(32):
+            total = total + jnp.where(pair == float(i), read[48 * i : 48 * i + 48], 0.0)
+        total = jnp.where(quarter_row == quarter, total, 0.0)
+        painted = jnp.dot(to_class, total.astype(jnp.bfloat16), preferred_element_type=jnp.float32)
+        gate = jax.nn.sigmoid(painted)
+        gate_high, gate_low = split(gate)
+        features = jnp.concatenate([chosen.astype(jnp.bfloat16), gate_high, gate_low], axis=0)
+        both = jnp.dot(wk_both, features, preferred_element_type=jnp.float32)
+        hidden = jnp.maximum(both[:64] + both[64:], 0.0)
+        row = jnp.floor(cell * (1.0 / 128.0))
+        col = cell - 128.0 * row
+        row = jnp.where(used > 0.5, row, -1.0)
+        by_row = jnp.concatenate(
+            [jnp.where(row == float(r), hidden, 0.0) for r in range(3)], axis=0
+        ).astype(jnp.bfloat16)
+        return lax.dot_general(
+            where_bf16(low_row == col), by_row, (((1,), (1,)), ((), ())),
+            preferred_element_type=jnp.float32,
+        )
+
+    for f in range(2):
+        pooled[f] = contribution(f, packed_first, 8 * f)
+    for f in range(2):
         most = jnp.max(jnp.maximum(place[2 * f], place[2 * f + 1])) + 1.0
         passes = (most.astype(jnp.int32) + SLOTS - 1) // SLOTS
-        packed[...] = packed_first[pl.ds(8 * f, 8)]
-        pooled[...] = jnp.zeros_like(pooled)
-
-        def one_pass(number, inner):
-            @pl.when(number > 0)
-            def _():
-                def group(g, state):
-                    pack_group(points, place, packed, f, g, (number * SLOTS).astype(jnp.float32), g)
-                    return state
-
-                lax.fori_loop(0, 8, group, 0)
-
-            def lanes(s, state):
-                chosen = jnp.concatenate([packed[2 * s], packed[2 * s + 1]], axis=1)
-                value = chosen[:8] + chosen[8:]
-                pixel, cell, used = value[4:5], value[5:6] - first_cell, value[6:7]
-                block = jnp.floor(pixel * (1.0 / 128.0))
-                low = pixel - 128.0 * block
-                pair = jnp.floor(block * 0.25)
-                quarter = block - 4.0 * pair
-                of_frame = jnp.concatenate([table[pl.ds(pl.multiple_of((2 * i + f) * 48, 48), 48), :] for i in range(32)], axis=0)
-                read = jnp.dot(of_frame, where_bf16(low_row == low), preferred_element_type=jnp.float32)
-                total = jnp.zeros((48, LANES), jnp.float32)
-                for i in range(32):
-                    total = total + jnp.where(pair == float(i), read[48 * i : 48 * i + 48], 0.0)
-                total = jnp.where(quarter_row == quarter, total, 0.0)
-                painted = jnp.dot(to_class, total.astype(jnp.bfloat16), preferred_element_type=jnp.float32)
-                gate = jax.nn.sigmoid(painted)
-                gate_high, gate_low = split(gate)
-                features = jnp.concatenate([chosen.astype(jnp.bfloat16), gate_high, gate_low], axis=0)
-                both = jnp.dot(wk_both, features, preferred_element_type=jnp.float32)
-                hidden = jnp.maximum(both[:64] + both[64:], 0.0)
-                row = jnp.floor(cell * (1.0 / 128.0))
-                col = cell - 128.0 * row
-                row = jnp.where(used > 0.5, row, -1.0)
-                by_row = jnp.concatenate(
-                    [jnp.where(row == float(r), hidden, 0.0) for r in range(3)], axis=0
-                ).astype(jnp.bfloat16)
-                pooled[...] += lax.dot_general(
-                    where_bf16(low_row == col), by_row, (((1,), (1,)), ((), ())),
-                    preferred_element_type=jnp.float32,
-                )
+
+        def one_pass(number, carry):
+            def group(g, state):
+                pack_group(points, place, packed, f, g, (number * SLOTS).astype(jnp.float32), g)
                 return state
 
-            lax.fori_loop(0, 8 * SLOTS // LANES, lanes, 0)
-            return inner
-
-        lax.fori_loop(0, passes, one_pass, 0)
-        grid = pooled[...]
+            lax.fori_loop(0, 8, group, 0)
+            pooled[f] += contribution(f, packed, 0)
+            return carry
+
+        lax.fori_loop(1, passes, one_pass, 0)
+    for f in range(2):
+        grid = pooled[f]
         total = None
         for d in range(3):
             if d == 0:
@@ -523,20 +525,16 @@
             part = jnp.dot(moved.astype(jnp.bfloat16), weight, preferred_element_type=jnp.float32)
             total = part if total is None else total + part
         feature = jnp.maximum(total, 0.0).astype(jnp.bfloat16)
-        found[f] = lax.dot_general(
+        out[:, f, :] = lax.dot_general(
             head[...], feature, (((1,), (1,)), ((), ())), preferred_element_type=jnp.float32
         )
-        return carry
-
-    lax.fori_loop(0, 2, frame, 0)
-    for f in range(2):
-        out[:, f, :] = found[f]
+    for f in range(2):
         for half in range(2):
             even, odd = sc[f, 11 * half : 11 * half + 11, :], sc[f, 11 * half + 22 : 11 * half + 33, :]
             scores[:, f, 128 * half : 128 * half + 128] = jnp.where(w % 2 == 0, even, odd)
 
 
-def point_part(points, table, packed, place, sc, wk, bev, head):
+def point_part(points, table, packed, place, sc, pillar, bev, head):
     vmem = pl.BlockSpec(memory_space=pltpu.VMEM)
     return pl.pallas_call(
         point_kernel,
@@ -549,12 +547,12 @@
         out_specs=(vmem, vmem),
         scratch_shapes=[
             pltpu.VMEM((8, 16, SLOTS), jnp.float32),
-            pltpu.VMEM((128, 192), jnp.float32),
-            pltpu.VMEM((2, 20, 128), jnp.float32),
+            pltpu.VMEM((2, 128, 192), jnp.float32),
+            pltpu.VMEM((128, 128), jnp.float32),
         ],
         compiler_params=pltpu.CompilerParams(vmem_limit_bytes=40 * 2**20),
         cost_estimate=pl.CostEstimate(flops=10**9, bytes_accessed=3 * 10**6, transcendentals=10**5),
-    )(points, table, packed, place, sc, wk, bev, head)
+    )(points, table, packed, place, sc, pillar, bev, head)
 
 
 def local(
@@ -572,10 +570,7 @@
     sc, table, points, packed, place = image_part(
         image, conv_weight, class_weight, point_feats, pixel_index, pillar_index, point_counts
     )
-    raw, gates = pillar_weight[:, :4], jnp.pad(pillar_weight[:, 4:], ((0, 0), (0, 5)))
-    raw = jnp.pad(raw, ((0, 0), (0, 4)))
-    wk = jnp.concatenate([raw, raw, gates, gates], axis=1)
-    detections, scores = point_part(points, table, packed, place, sc, wk, bev_weight, head_weight.T)
+    detections, scores = point_part(points, table, packed, place, sc, pillar_weight.T, bev_weight, head_weight.T)
     return (detections.transpose(1, 2, 0), scores.transpose(1, 0, 2))
 
 

time: 87.9 us -> 82 us (0.933)
  Pallas kernels: 84.7 us -> 81.2 us
  local copies, waits for them, and re-layouts: 1.59 us -> 0.01 us
    pallas_call x1, Pallas kernels: 9 us -> 4.41 us  [point_part(): pl.pallas_call(point_kernel, name='point_part', out_shape=(jax.ShapeDtype...]
    slice x3 -> x0, local copies, waits for them, and re-layouts: 1.47 us -> none
    pallas_call x1, Pallas kernels: 75.6 us -> 76.8 us  [image_part(): pl.pallas_call(image_kernel, name='image_part', out_shape=(jax.ShapeDtype...]
where the time goes in v4:
time: 82 us; the launch traced here: 81.9 us
  Pallas kernels  81.2 us (99%)
    pallas_call x1, Pallas kernels, image_part(): pl.pallas_call(image_kernel, name='image_part', out_shape=(jax.ShapeDtype...  76.8 us
    pallas_call x1, Pallas kernels, point_part(): pl.pallas_call(point_kernel, name='point_part', out_shape=(jax.ShapeDtype...  4.41 us

profile of v4, /device:TPU:8, one launch (start us, length us, event | category | flops | bytes accessed | tf_op | source)
XLA Modules:
  0.0 81.9 jit_solution(8297569343418322036)
XLA Ops:
  0.6 0.0 copy-start
  0.6 0.0 copy-start.1
  0.7 0.0 copy-start.2
  0.7 76.8 %image_part.1 = (f32[2,48,128]{2,1,0:T(8,128)S(1)}, bf16[3072,128]{1,0:T(8,128)(2,1)S(1)}, f32[2048,128]{1,0:T(8,128)S(1)}, f32[16,16,128]{2,1,0:T(8,128)S(1)}, f32[4,64,128]{2,1,0:T(8,128)S(1)}) custom-call(bf16[16,256,256]{2,1,0:T(8,128)(2,1)} %image.1, bf16[1,256,2304]{2,1,0:T(8,128)(2,1)} %w_own.1, bf16[11,256]{1,0:T(8,128)(2,1)} %class_weight_h.1, ...), custom_call_target="tpu_custom_call" | custom-call | flops 10000000000 | bytes 10000000 | tf_op jit(solution)/shard_map/image_part/pallas_call | solution.py:417
  77.5 0.0 copy-done
  77.5 0.0 copy-done.1
  77.5 0.0 copy-done.2
  77.5 4.4 %point_part.1 = (f32[20,2,128]{2,1,0:T(2,128)}, f32[11,2,256]{2,1,0:T(2,128)}) custom-call(f32[2048,128]{1,0:T(8,128)S(1)} %get-tuple-element.9.points, bf16[3072,128]{1,0:T(8,128)(2,1)S(1)} %get-tuple-element.10.table, f32[16,16,128]{2,1,0:T(8,128)S(1)} %get-tuple-element.11.packed_first, f32[4,64,128]{2,1,0:T(8,128)S(1)} %get-tuple-element.12.place, ...), custom_call_target="tpu_custom_call" | custom-call | flops 1000000000 | bytes 3000000 | tf_op jit(solution)/shard_map/point_part/pallas_call | solution.py:539
Async XLA Ops:
  0.6 76.8 %copy-start = (bf16[576,384]{1,0:T(8,128)(2,1)S(1)}, bf16[576,384]{1,0:T(8,128)(2,1)}, u32[]{:S(2)}) copy-start(bf16[576,384]{1,0:T(8,128)(2,1)} %bev.1) | copy-start | bytes 1327108
  0.6 76.8 %copy-start.1 = (bf16[384,20]{0,1:T(8,128)(2,1)S(1)}, bf16[384,20]{0,1:T(8,128)(2,1)}, u32[]{:S(2)}) copy-start(bf16[384,20]{0,1:T(8,128)(2,1)} %param.19) | copy-start | bytes 46084
  0.7 76.8 %copy-start.2 = (f32[64,15]{0,1:T(8,128)S(1)}, f32[64,15]{0,1:T(8,128)}, u32[]{:S(2)}) copy-start(f32[64,15]{0,1:T(8,128)} %param.17) | copy-start | bytes 11524

commit v5 on v4

--- a/solution.py
+++ b/solution.py
@@ -12,8 +12,8 @@
 MOST_ROWS = 12
 MESH = pl.DeviceIdType.MESH
 NEAR = (4, -4, 3, -3, 2, -2, 1, -1)
-EARLY = (0, 4, -4, 1, -1, 2, -2, 3, -3)
-LATE = (5, -5, 6, -6, 7, -7, 8)
+BATCHES = ((3, 9), (12, 4), (0, 3))
+PASSED_ON = (((3, 5), (8, 4)), ((12, 4), None), (None, (0, 3)))
 
 
 SLOTS = 128
@@ -142,12 +142,13 @@
         pl.semaphore_signal(barrier, inc=1, device_id=peer, device_id_type=MESH)
     for copy in small:
         copy.wait()
+    own_slot = 16 * x + 7
     lane = lax.broadcasted_iota(jnp.int32, (1, 256), 1)
     for f in range(2):
         cell = jnp.where(lane < counts[:, f : f + 1], pillar[f : f + 1, :], -1024).astype(jnp.float32)
         where = pixel[f : f + 1, :].astype(jnp.float32)
         for h in range(2):
-            first = 32 * w + (2 * f + h) * 8
+            first = 32 * own_slot + (2 * f + h) * 8
             points[pl.ds(first, 4), :] = feats[f, :, 128 * h : 128 * h + 128]
             points[pl.ds(first + 4, 1), :] = where[:, 128 * h : 128 * h + 128]
             points[pl.ds(first + 5, 1), :] = cell[:, 128 * h : 128 * h + 128]
@@ -181,9 +182,9 @@
     for d, f in halo_peers:
         send(img.at[f], block(2 - 2 * d + t), h_sem.at[2 - 2 * d + t], at(p, (2 * (k + d) + f + 64) % 64))
 
-    def post(src, sem, number, device):
+    def post(src, dst, sem, number, device):
         pltpu.make_async_remote_copy(
-            src_ref=src, dst_ref=src, send_sem=ag_send.at[number], recv_sem=sem,
+            src_ref=src, dst_ref=dst, send_sem=ag_send.at[number], recv_sem=sem,
             device_id=device, device_id_type=MESH,
         ).start()
 
@@ -192,43 +193,48 @@
             self.ref, self.rows, self.number = ref, rows, number
             self.z_sem, self.x_sem, self.f_sem = z_sem, x_sem, f_sem
 
-        def block(self, d, column=0):
-            return self.some(16 * ((x + column + 4) % 4) + (z - d + 16) % 16, 1)
-
-        def some(self, first, count):
+        def some(self, slot, count, column=0):
+            first = 16 * ((x + column + 4) % 4) + slot
             return self.ref.at[pl.ds(pl.multiple_of(self.rows * first, self.rows), self.rows * count)]
+
+        def block(self, d):
+            return self.some(d + 7, 1)
 
         def z_first(self):
             for d in NEAR:
-                post(self.block(0), self.z_sem.at[d % 16], self.number, z_dev(d))
-
-        def z_wait(self, d):
-            arrived(self.block(d), self.z_sem.at[d % 16])
+                post(self.block(0), self.block(d), self.z_sem.at[d + 7], self.number, z_dev(d))
+
+        def z_wait(self, *distances):
+            for d in distances:
+                arrived(self.block(d), self.z_sem.at[d + 7])
 
         def z_second(self):
             for d in (4, -4):
                 self.z_wait(d)
                 for e in (4, 3, 2, 1) if d > 0 else (-3, -2, -1):
-                    post(self.block(d), self.z_sem.at[(d + e) % 16], self.number, z_dev(e))
-
-        def x_first(self, d):
+                    post(self.block(d), self.block(d + e), self.z_sem.at[d + e + 7], self.number, z_dev(e))
+
+        def x_first(self, batch):
+            ref = self.some(*BATCHES[batch])
             for side in range(2):
-                post(self.block(d), self.x_sem.at[side, d % 16], self.number, x_dev(1 - 2 * side))
-
-        def x_second(self, d):
+                post(ref, ref, self.x_sem.at[side, batch], self.number, x_dev(1 - 2 * side))
+
+        def x_second(self, batch):
             for side in range(2):
                 step = 1 - 2 * side
-                arrived(self.block(d, -step), self.x_sem.at[side, d % 16])
-                if d % 2 == side:
-                    post(self.block(d, -step), self.f_sem, self.number, x_dev(step))
+                arrived(self.some(*BATCHES[batch], -step), self.x_sem.at[side, batch])
+                if PASSED_ON[batch][side]:
+                    ref = self.some(*PASSED_ON[batch][side], -step)
+                    post(ref, ref, self.f_sem, self.number, x_dev(step))
 
         def last(self):
-            arrived(self.some(16 * ((x + 2) % 4), 16), self.f_sem)
+            arrived(self.some(0, 16, 2), self.f_sem)
 
         def sent(self):
+            ref = self.ref.at[pl.ds(0, 63 * self.rows)]
             pltpu.make_async_remote_copy(
-                src_ref=self.some(0, 63), dst_ref=self.some(0, 63),
-                send_sem=ag_send.at[self.number], recv_sem=own_sem, device_id=partner, device_id_type=MESH,
+                src_ref=ref, dst_ref=ref, send_sem=ag_send.at[self.number], recv_sem=own_sem,
+                device_id=partner, device_id_type=MESH,
             ).wait_send()
 
     spread_points = Spread(points, 32, pz_sem, px_sem, pf_sem, 0)
@@ -334,17 +340,16 @@
     layer(0)
     layer(1)
     x_second(late_layer, late)
-    for d in EARLY + LATE:
-        if d not in (0, 4, -4):
-            spread_points.z_wait(d)
-        spread_points.x_first(d)
+    spread_points.z_wait(1, -1, 2, -2, 3, -3, 5, 6, 7, 8, -5, -6, -7)
+    for batch in range(3):
+        spread_points.x_first(batch)
     layer(2)
     x_done(late_layer, late)
     hand_over(late_layer, 1)
     layer(3)
     layer(4)
-    for d in EARLY + LATE:
-        spread_points.x_second(d)
+    for batch in range(3):
+        spread_points.x_second(batch)
     layer(5)
     layer(6)
     layer(7)
@@ -364,10 +369,9 @@
             preferred_element_type=jnp.float32,
         )
         total = part if total is None else total + part
-    table[pl.ds(pl.multiple_of(48 * w, 48), 48), :] = total.astype(jnp.bfloat16)
+    table[pl.ds(pl.multiple_of(48 * own_slot, 48), 48), :] = total.astype(jnp.bfloat16)
     sc[t] = total
     spread_table.z_first()
-    spread_table.x_first(0)
     send(sc.at[t], sc.at[t], s_sem, sibling)
     spread_points.last()
     first_cell = ((w - 1) * 128).astype(jnp.float32)
@@ -381,22 +385,19 @@
 
         lax.fori_loop(first, last, one, 0)
 
-    pack(0, 4)
+    pack(0, 6)
     spread_table.z_second()
-    spread_table.x_first(4)
-    spread_table.x_first(-4)
-    for d in (1, -1, 2, -2, 3, -3):
-        spread_table.z_wait(d)
-        spread_table.x_first(d)
-    pack(4, 8)
-    for d in EARLY:
-        spread_table.x_second(d)
-    for d in LATE:
-        spread_table.z_wait(d)
-        spread_table.x_first(d)
-    pack(8, 16)
-    for d in LATE:
-        spread_table.x_second(d)
+    spread_table.z_wait(1, -1, 2, -2, 3, -3)
+    spread_table.x_first(0)
+    pack(6, 12)
+    spread_table.x_second(0)
+    spread_table.z_wait(5, 6, 7, 8)
+    spread_table.x_first(1)
+    spread_table.z_wait(-5, -6, -7)
+    spread_table.x_first(2)
+    pack(12, 16)
+    spread_table.x_second(1)
+    spread_table.x_second(2)
     spread_points.sent()
     spread_table.last()
     spread_table.sent()
@@ -437,7 +438,7 @@
             pltpu.VMEM((2, 256), jnp.int32),
             pltpu.VMEM((1, 2), jnp.int32),
             dma, dma, dma((5,)), dma((N_SENDS,)), dma((6,)), dma((2, 3)), dma((2, 2)), dma((2, 3)), dma((2, 3)), dma((4, 2)),
-            dma((16,)), dma((2, 16)), dma, dma((16,)), dma((2, 16)), dma, dma, dma((2,)),
+            dma((16,)), dma((2, 3)), dma, dma((16,)), dma((2, 3)), dma, dma, dma((2,)),
         ],
         compiler_params=pltpu.CompilerParams(
             collective_id=0, has_side_effects=True, vmem_limit_bytes=40 * 2**20
@@ -448,6 +449,7 @@
 
 def point_kernel(points, table, packed_first, place, sc, pillar, bev, head, out, scores, packed, pooled, spare):
     w = lax.axis_index("wide")
+    z = w % 16
     first_cell = ((w - 1) * 128).astype(jnp.float32)
     low_row = iota((128, LANES), 0)
     quarter_row = lax.broadcasted_iota(jnp.int32, (48, LANES), 0) // 11
@@ -472,11 +474,14 @@
         low = pixel - 128.0 * block
         pair = jnp.floor(block * 0.25)
         quarter = block - 4.0 * pair
-        of_frame = jnp.concatenate([table[pl.ds(pl.multiple_of((2 * i + f) * 48, 48), 48), :] for i in range(32)], axis=0)
+        odd = (z + 1 + f) % 2
+        rows = [pl.multiple_of(48 * (16 * i + 2 * j + odd), 48) for i in range(4) for j in range(8)]
+        of_frame = jnp.concatenate([table[pl.ds(first_row, 48), :] for first_row in rows], axis=0)
+        pairs = [8 * i + (z + 23 - 2 * j - odd) % 16 // 2 for i in range(4) for j in range(8)]
         read = jnp.dot(of_frame, where_bf16(low_row == low), preferred_element_type=jnp.float32)
         total = jnp.zeros((48, LANES), jnp.float32)
         for i in range(32):
-            total = total + jnp.where(pair == float(i), read[48 * i : 48 * i + 48], 0.0)
+            total = total + jnp.where(pair == pairs[i].astype(jnp.float32), read[48 * i : 48 * i + 48], 0.0)
         total = jnp.where(quarter_row == quarter, total, 0.0)
         painted = jnp.dot(to_class, total.astype(jnp.bfloat16), preferred_element_type=jnp.float32)
         gate = jax.nn.sigmoid(painted)

time: 82 us -> 81.2 us (level)
  Pallas kernels: 81.2 us -> 80.3 us
    pallas_call x1, Pallas kernels: 76.8 us -> 75.9 us  [image_part(): pl.pallas_call(image_kernel, name='image_part', out_shape=(jax.ShapeDtype...]
where the time goes in v5:
time: 81.2 us; the launch traced here: 81 us
  Pallas kernels  80.3 us (99%)
    pallas_call x1, Pallas kernels, image_part(): pl.pallas_call(image_kernel, name='image_part', out_shape=(jax.ShapeDtype...  75.9 us
    pallas_call x1, Pallas kernels, point_part(): pl.pallas_call(point_kernel, name='point_part', out_shape=(jax.ShapeDtype...  4.43 us

profile of v5, /device:TPU:8, one launch (start us, length us, event | category | flops | bytes accessed | tf_op | source)
XLA Modules:
  0.0 81.0 jit_solution(16506127617565193263)
XLA Ops:
  0.6 0.0 copy-start
  0.6 0.0 copy-start.1
  0.7 0.0 copy-start.2
  0.7 75.9 %image_part.1 = (f32[2,48,128]{2,1,0:T(8,128)S(1)}, bf16[3072,128]{1,0:T(8,128)(2,1)S(1)}, f32[2048,128]{1,0:T(8,128)S(1)}, f32[16,16,128]{2,1,0:T(8,128)S(1)}, f32[4,64,128]{2,1,0:T(8,128)S(1)}) custom-call(bf16[16,256,256]{2,1,0:T(8,128)(2,1)} %image.1, bf16[1,256,2304]{2,1,0:T(8,128)(2,1)} %w_own.1, bf16[11,256]{1,0:T(8,128)(2,1)} %class_weight_h.1, ...), custom_call_target="tpu_custom_call" | custom-call | flops 10000000000 | bytes 10000000 | tf_op jit(solution)/shard_map/image_part/pallas_call | solution.py:418
  76.5 0.0 copy-done
  76.6 0.0 copy-done.1
  76.6 0.0 copy-done.2
  76.6 4.4 %point_part.1 = (f32[20,2,128]{2,1,0:T(2,128)}, f32[11,2,256]{2,1,0:T(2,128)}) custom-call(f32[2048,128]{1,0:T(8,128)S(1)} %get-tuple-element.9.points, bf16[3072,128]{1,0:T(8,128)(2,1)S(1)} %get-tuple-element.10.table, f32[16,16,128]{2,1,0:T(8,128)S(1)} %get-tuple-element.11.packed_first, f32[4,64,128]{2,1,0:T(8,128)S(1)} %get-tuple-element.12.place, ...), custom_call_target="tpu_custom_call" | custom-call | flops 1000000000 | bytes 3000000 | tf_op jit(solution)/shard_map/point_part/pallas_call | solution.py:544
Async XLA Ops:
  0.6 75.9 %copy-start = (bf16[576,384]{1,0:T(8,128)(2,1)S(1)}, bf16[576,384]{1,0:T(8,128)(2,1)}, u32[]{:S(2)}) copy-start(bf16[576,384]{1,0:T(8,128)(2,1)} %bev.1) | copy-start | bytes 1327108
  0.6 75.9 %copy-start.1 = (bf16[384,20]{0,1:T(8,128)(2,1)S(1)}, bf16[384,20]{0,1:T(8,128)(2,1)}, u32[]{:S(2)}) copy-start(bf16[384,20]{0,1:T(8,128)(2,1)} %param.19) | copy-start | bytes 46084
  0.7 75.9 %copy-start.2 = (f32[64,15]{0,1:T(8,128)S(1)}, f32[64,15]{0,1:T(8,128)}, u32[]{:S(2)}) copy-start(f32[64,15]{0,1:T(8,128)} %param.17) | copy-start | bytes 11524

commit v6 on v5

--- a/solution.py
+++ b/solution.py
@@ -259,9 +259,24 @@
     late = 1 - soon
     soon_layer, late_layer = layer_of(soon_step), layer_of(-soon_step)
 
+    def hand_over(layer):
+        part = weights.at[layer, :, pl.ds(0, 768)]
+        send(part, part, d_sem.at[layer // 2, 4], partner)
+
+    def hand_quarter(layer, owner):
+        send(q_cols(layer, owner), q_cols(layer, owner), d_sem.at[layer // 2, owner], partner)
+
+    def taken_over(number):
+        @pl.when(c == 1 - number % 2)
+        def _():
+            arrived(weights.at[number, :, pl.ds(0, 768)], d_sem.at[number // 2, 4])
+            for owner in range(4):
+                arrived(q_cols(number, owner), d_sem.at[number // 2, owner])
+
     def x_first(layer, j):
         for d in range(2):
             send(q_cols(layer, x), q_cols(layer, x), x1_sem.at[d, j], x_dev(steps[d]))
+        hand_quarter(layer, x)
 
     def x_second(layer, j):
         for d in range(2):
@@ -269,26 +284,19 @@
             arrived(q_cols(layer, source), x1_sem.at[d, j])
             part = q_cols(layer, source, *q_parts[d])
             send(part, part, x2_sem.at[d, j], x_dev(steps[d]))
+            hand_quarter(layer, source)
 
     def x_done(layer, j):
         for d in range(2):
             arrived(q_cols(layer, (x + 2) % 4, *q_parts[d]), x2_sem.at[d, j])
-
-    def hand_over(layer, half):
-        part = weights.at[layer, :, pl.ds(768 * half, 768 + 768 * half)]
-        send(part, part, d_sem.at[layer // 2, half], partner)
-
-    def taken_over(number):
-        @pl.when(c == 1 - number % 2)
-        def _():
-            for half in range(2):
-                arrived(weights.at[number, :, pl.ds(768 * half, 768 + 768 * half)], d_sem.at[number // 2, half])
+        hand_quarter(layer, (x + 2) % 4)
 
     own_copy.wait()
     for d in range(2):
         send(q_cols(p, x), q_cols(p, x), y1_sem.at[d, 0], y_dev(steps[d]))
-    hand_over(p, 0)
-    hand_over(p, 1)
+    hand_over(p)
+    for owner in range(4):
+        hand_quarter(p, owner)
     spread_points.z_first()
     for d in range(2):
         arrived(q_cols(near[d], x), y1_sem.at[d, 0])
@@ -309,16 +317,14 @@
     x_first(late_layer, late)
     for d in range(2):
         arrived(a_cols(far, d), y2_sem.at[d, 1])
-    hand_over(far, 0)
+    hand_over(far)
     spread_points.z_second()
     for d in range(2):
         arrived(a_cols(near[d], 1 - d), y1_sem.at[d, 2])
-    hand_over(soon_layer, 0)
-    hand_over(late_layer, 0)
+    hand_over(soon_layer)
+    hand_over(late_layer)
     x_done(soon_layer, soon)
-    hand_over(soon_layer, 1)
     x_done(far, 2)
-    hand_over(far, 1)
 
     act[0, pl.ds(pl.multiple_of((2 + t) * 256, 256), 256), :] = img[t]
     for j in (0, 1, 4, 5):
@@ -345,7 +351,6 @@
         spread_points.x_first(batch)
     layer(2)
     x_done(late_layer, late)
-    hand_over(late_layer, 1)
     layer(3)
     layer(4)
     for batch in range(3):
@@ -406,7 +411,7 @@
         copy.wait_send()
 
 
-N_SENDS = 48
+N_SENDS = 52
 
 
 def image_part(image, conv_weight, class_weight, feats, pixel, pillar, counts):
@@ -437,7 +442,7 @@
             pltpu.VMEM((2, 256), jnp.int32),
             pltpu.VMEM((2, 256), jnp.int32),
             pltpu.VMEM((1, 2), jnp.int32),
-            dma, dma, dma((5,)), dma((N_SENDS,)), dma((6,)), dma((2, 3)), dma((2, 2)), dma((2, 3)), dma((2, 3)), dma((4, 2)),
+            dma, dma, dma((5,)), dma((N_SENDS,)), dma((6,)), dma((2, 3)), dma((2, 2)), dma((2, 3)), dma((2, 3)), dma((4, 5)),
             dma((16,)), dma((2, 3)), dma, dma((16,)), dma((2, 3)), dma, dma, dma((2,)),
         ],
         compiler_params=pltpu.CompilerParams(

time: 81.2 us -> 80.7 us (level)
  no operation moved by 1% of the time
where the time goes in v6:
time: 80.7 us; the launch traced here: 80.6 us
  Pallas kernels  79.9 us (99%)
    pallas_call x1, Pallas kernels, image_part(): pl.pallas_call(image_kernel, name='image_part', out_shape=(jax.ShapeDtype...  75.4 us
    pallas_call x1, Pallas kernels, point_part(): pl.pallas_call(point_kernel, name='point_part', out_shape=(jax.ShapeDtype...  4.43 us

profile of v6, /device:TPU:8, one launch (start us, length us, event | category | flops | bytes accessed | tf_op | source)
XLA Modules:
  0.0 80.6 jit_solution(15517431500762970359)
XLA Ops:
  0.6 0.0 copy-start
  0.6 0.0 copy-start.1
  0.7 0.0 copy-start.2
  0.7 75.4 %image_part.1 = (f32[2,48,128]{2,1,0:T(8,128)S(1)}, bf16[3072,128]{1,0:T(8,128)(2,1)S(1)}, f32[2048,128]{1,0:T(8,128)S(1)}, f32[16,16,128]{2,1,0:T(8,128)S(1)}, f32[4,64,128]{2,1,0:T(8,128)S(1)}) custom-call(bf16[16,256,256]{2,1,0:T(8,128)(2,1)} %image.1, bf16[1,256,2304]{2,1,0:T(8,128)(2,1)} %w_own.1, bf16[11,256]{1,0:T(8,128)(2,1)} %class_weight_h.1, ...), custom_call_target="tpu_custom_call" | custom-call | flops 10000000000 | bytes 10000000 | tf_op jit(solution)/shard_map/image_part/pallas_call | solution.py:423
  76.1 0.0 copy-done
  76.1 0.0 copy-done.1
  76.1 0.0 copy-done.2
  76.1 4.4 %point_part.1 = (f32[20,2,128]{2,1,0:T(2,128)}, f32[11,2,256]{2,1,0:T(2,128)}) custom-call(f32[2048,128]{1,0:T(8,128)S(1)} %get-tuple-element.9.points, bf16[3072,128]{1,0:T(8,128)(2,1)S(1)} %get-tuple-element.10.table, f32[16,16,128]{2,1,0:T(8,128)S(1)} %get-tuple-element.11.packed_first, f32[4,64,128]{2,1,0:T(8,128)S(1)} %get-tuple-element.12.place, ...), custom_call_target="tpu_custom_call" | custom-call | flops 1000000000 | bytes 3000000 | tf_op jit(solution)/shard_map/point_part/pallas_call | solution.py:549
Async XLA Ops:
  0.6 75.5 %copy-start = (bf16[576,384]{1,0:T(8,128)(2,1)S(1)}, bf16[576,384]{1,0:T(8,128)(2,1)}, u32[]{:S(2)}) copy-start(bf16[576,384]{1,0:T(8,128)(2,1)} %bev.1) | copy-start | bytes 1327108
  0.6 75.5 %copy-start.1 = (bf16[384,20]{0,1:T(8,128)(2,1)S(1)}, bf16[384,20]{0,1:T(8,128)(2,1)}, u32[]{:S(2)}) copy-start(bf16[384,20]{0,1:T(8,128)(2,1)} %param.19) | copy-start | bytes 46084
  0.7 75.5 %copy-start.2 = (f32[64,15]{0,1:T(8,128)S(1)}, f32[64,15]{0,1:T(8,128)}, u32[]{:S(2)}) copy-start(f32[64,15]{0,1:T(8,128)} %param.17) | copy-start | bytes 11524
